TPU v7x, 32 devices: a whole 2x2x4 slice. The times are simulated.
32 devices in a mesh: cells: 8 (over z, x), genes: 4 (over y, core).
Axes of the slice: x: 2, y: 2, z: 4, core: 2. Of those that a mesh axis runs over, the one named last changes fastest.
Arguments:
- counts: int32 [38912, 4000], P('cells', 'genes'), may hold values from 0 to 674, as said below
- sketch: bfloat16 [4000, 128], P('genes'), may hold values from -6 to 6
Outputs:
- basis: float32 [38912, 128], P('cells')
- loadings: float32 [4000, 128], P('genes')
Inputs may be any that keep to these rules, and one draw needn't show every extreme that they name: `counts`: every cell and every gene has a positive total.
All inputs are finite; a program needn't handle non-finite values.
Results may differ from a plain program's by a relative error of at most 0.0051.
Values may be sent and summed in bfloat16 or wider, within the bound.
A program may use at most 128 MiB of HBM per device.

v0:
```python
import functools
import math

import jax
import jax.numpy as jnp
from jax import lax
from jax.experimental import pallas as pl
from jax.experimental.pallas import tpu as pltpu
from jax.sharding import PartitionSpec as P

ITERS = 2
MESH = pl.DeviceIdType.MESH


def greet(peers):
    barrier = pltpu.get_barrier_semaphore()
    for peer in peers:
        pl.semaphore_signal(barrier, inc=1, device_id=peer, device_id_type=MESH)
    pl.semaphore_wait(barrier, len(peers))


def ring_peers(axis, count):
    me = lax.axis_index(axis)
    return [{axis: lax.rem(me + step, count)} for step in range(1, count)]


def send(src, dst, sems, slot, peer):
    copy = pltpu.make_async_remote_copy(
        src_ref=src,
        dst_ref=dst,
        send_sem=sems.at[0, slot],
        recv_sem=sems.at[1, slot],
        device_id=peer,
        device_id_type=MESH,
    )
    copy.start()
    return copy


def sems(count):
    return pltpu.SemaphoreType.DMA((2, max(count, 1)))


def remote_call(body, out_shape, scratch, ident):
    leaves = jax.tree.leaves(out_shape)
    specs = [pl.BlockSpec(memory_space=pltpu.VMEM)] * len(leaves)

    def call(*args):
        return pl.pallas_call(
            body,
            out_shape=out_shape,
            in_specs=[pl.BlockSpec(memory_space=pltpu.VMEM)] * len(args),
            out_specs=specs if isinstance(out_shape, (list, tuple)) else specs[0],
            scratch_shapes=scratch,
            compiler_params=pltpu.CompilerParams(
                collective_id=ident, has_side_effects=True, vmem_limit_bytes=16 * 1024 * 1024
            ),
        )(*args)

    return call


def totals_body(n, m, gene_ref, cell_ref, gene_out, cell_out, grand_out, gene_buf, cell_buf, row, row_buf, gene_sem, cell_sem, row_sem):
    cell_peers = ring_peers("cells", n)
    gene_peers = ring_peers("genes", m)
    greet(cell_peers + gene_peers)
    gene_copies = [send(gene_ref, gene_buf.at[i], gene_sem, i, peer) for i, peer in enumerate(cell_peers)]
    cell_copies = [send(cell_ref, cell_buf.at[i], cell_sem, i, peer) for i, peer in enumerate(gene_peers)]
    total = gene_ref[...]
    for i, copy in enumerate(gene_copies):
        copy.wait_recv()
        total = total + gene_buf[i]
    gene_out[...] = total
    row[...] = jnp.broadcast_to(jnp.sum(total, axis=0, keepdims=True), row.shape)
    row_copies = [send(row, row_buf.at[i], row_sem, i, peer) for i, peer in enumerate(gene_peers)]
    total = cell_ref[...]
    for i, copy in enumerate(cell_copies):
        copy.wait_recv()
        total = total + cell_buf[i]
    cell_out[...] = total
    total = row[...]
    for i, copy in enumerate(row_copies):
        copy.wait_recv()
        total = total + row_buf[i]
    grand_out[...] = total
    for copy in gene_copies + cell_copies + row_copies:
        copy.wait_send()


def all_totals(gene_part, cell_part, n, m, ident):
    f32 = jnp.float32
    return remote_call(
        functools.partial(totals_body, n, m),
        [
            jax.ShapeDtypeStruct(gene_part.shape, f32),
            jax.ShapeDtypeStruct(cell_part.shape, f32),
            jax.ShapeDtypeStruct((8, 128), f32),
        ],
        [
            pltpu.VMEM((n - 1,) + gene_part.shape, f32),
            pltpu.VMEM((m - 1,) + cell_part.shape, f32),
            pltpu.VMEM((8, 128), f32),
            pltpu.VMEM((m - 1, 8, 128), f32),
            sems(n - 1),
            sems(m - 1),
            sems(m - 1),
        ],
        ident,
    )(gene_part, cell_part)


def gene_places(m):
    me = lax.axis_index("genes")
    rows = m // 2
    core, row = lax.rem(me, 2), lax.div(me, 2)
    partner = {"genes": row * 2 + 1 - core}
    others = [lax.rem(row + step, rows) for step in range(1, rows)]
    return core, row, partner, others, [{"genes": other * 2 + core} for other in others]


def scatter_body(m, x_ref, out_ref, near, outgoing, far, near_sem, far_sem):
    core, row, partner, others, peers = gene_places(m)
    greet([partner] + peers)
    first = [send(x_ref.at[1 - core, other], near.at[other], near_sem, i, partner) for i, other in enumerate(others + [row])]
    second = []
    for i, other in enumerate(others):
        first[i].wait_recv()
        outgoing[i] = x_ref[core, other] + near[other]
        second.append(send(outgoing.at[i], far.at[i], far_sem, i, peers[i]))
    first[-1].wait_recv()
    out_ref[...] = x_ref[core, row] + near[row]
    for i, copy in enumerate(second):
        copy.wait_recv()
        out_ref[...] += far[i]
    for copy in first + second:
        copy.wait_send()


def scatter_genes(x, m, ident):
    block = x.shape[0] // m
    rows = m // 2
    f32 = jnp.float32
    return remote_call(
        functools.partial(scatter_body, m),
        jax.ShapeDtypeStruct((block, x.shape[1]), f32),
        [
            pltpu.VMEM((rows, block, x.shape[1]), f32),
            pltpu.VMEM((max(rows - 1, 1), block, x.shape[1]), f32),
            pltpu.VMEM((max(rows - 1, 1), block, x.shape[1]), f32),
            sems(rows),
            sems(rows - 1),
        ],
        ident,
    )(x.reshape(2, rows, block, x.shape[1]))


def gather_body(m, x_ref, out_ref, far_sem, near_sem):
    core, row, partner, others, peers = gene_places(m)
    rows = m // 2
    greet([partner] + peers)
    mine = out_ref.at[core, row]
    out_ref[core, row] = x_ref[...]
    far = [send(x_ref, mine, far_sem, i, peer) for i, peer in enumerate(peers)]
    near = [send(x_ref, mine, near_sem, 0, partner)]
    for i in range(rows - 1):
        far[i].wait_recv()
        origin = lax.rem(row + rows - 1 - i, rows)
        near.append(send(out_ref.at[core, origin], out_ref.at[core, origin], near_sem, i + 1, partner))
    for copy in near:
        copy.wait_recv()
    for copy in far + near:
        copy.wait_send()


def gather_genes(x, m, ident):
    rows = m // 2
    out = remote_call(
        functools.partial(gather_body, m),
        jax.ShapeDtypeStruct((2, rows) + x.shape, x.dtype),
        [sems(rows - 1), sems(rows)],
        ident,
    )(x)
    return out.reshape(m * x.shape[0], x.shape[1])


def gram_body(n, m, x_ref, out_ref, buf, part, part_buf, first_sem, part_sem, last_sem):
    me = lax.axis_index("cells")
    cell_peers = ring_peers("cells", n)
    gene_peers = ring_peers("genes", m)
    greet(cell_peers + gene_peers)
    first = [send(x_ref.at[peer["cells"]], buf.at[i], first_sem, i, peer) for i, peer in enumerate(cell_peers)]
    total = x_ref[me]
    for i, copy in enumerate(first):
        copy.wait_recv()
        total = total + buf[i]
    part[...] = total
    middle = [send(part, part_buf.at[i], part_sem, i, peer) for i, peer in enumerate(gene_peers)]
    for i, copy in enumerate(middle):
        copy.wait_recv()
        total = total + part_buf[i]
    out_ref[me] = total
    last = [send(out_ref.at[me], out_ref.at[me], last_sem, i, peer) for i, peer in enumerate(cell_peers)]
    for copy in last:
        copy.wait_recv()
    for copy in first + middle + last:
        copy.wait_send()


def sum_gram(gram, n, m, ident):
    width = gram.shape[0]
    shape = (n, width // n, width)
    f32 = jnp.float32
    out = remote_call(
        functools.partial(gram_body, n, m),
        jax.ShapeDtypeStruct(shape, f32),
        [
            pltpu.VMEM((n - 1,) + shape[1:], f32),
            pltpu.VMEM(shape[1:], f32),
            pltpu.VMEM((m - 1,) + shape[1:], f32),
            sems(n - 1),
            sems(m - 1),
            sems(n - 1),
        ],
        ident,
    )(gram.reshape(shape))
    return out.reshape(width, width)


def loading_body(n, scale, x_ref, out_ref, buf, first_sem, last_sem):
    me = lax.axis_index("cells")
    peers = ring_peers("cells", n)
    greet(peers)
    first = [send(x_ref.at[peer["cells"]], buf.at[i], first_sem, i, peer) for i, peer in enumerate(peers)]
    total = x_ref[me]
    for i, copy in enumerate(first):
        copy.wait_recv()
        total = total + buf[i]
    out_ref[me] = (total * scale).astype(out_ref.dtype)
    last = [send(out_ref.at[me], out_ref.at[me], last_sem, i, peer) for i, peer in enumerate(peers)]
    for copy in last:
        copy.wait_recv()
    for copy in first + last:
        copy.wait_send()


def loading_total(partial_sum, scale, n, ident):
    genes, width = partial_sum.shape
    unit = 16 * n
    padded = -(-genes // unit) * unit
    shape = (n, padded // n, width)
    x = jnp.pad(partial_sum, ((0, padded - genes), (0, 0))).reshape(shape)
    out = remote_call(
        functools.partial(loading_body, n, scale),
        jax.ShapeDtypeStruct(shape, jnp.bfloat16),
        [pltpu.VMEM((n - 1,) + shape[1:], jnp.float32), sems(n - 1), sems(n - 1)],
        ident,
    )(x)
    return out.reshape(padded, width)[:genes]


def residual_block(block, cell_total, frac, limit):
    values = block.astype(jnp.float32)
    expected = cell_total[:, None] * frac[None, :]
    scaled = (values - expected) / jnp.sqrt(expected + 0.01 * expected * expected)
    return jnp.clip(scaled, -limit, limit).astype(jnp.bfloat16)


def self_gram(block):
    return lax.dot_general(
        block,
        block,
        (((0,), (0,)), ((), ())),
        precision=lax.Precision.HIGHEST,
        preferred_element_type=jnp.float32,
    )


def whiten_body(scale, gram_ref, out_ref, left, right):
    width = gram_ref.shape[0]
    eye = lax.broadcasted_iota(jnp.int32, (width, width), 0) == lax.broadcasted_iota(jnp.int32, (width, width), 1)
    gram = gram_ref[...]
    diagonal = jnp.where(eye, gram, 0.0)
    trace = jnp.sum(jnp.sum(diagonal, axis=1, keepdims=True), axis=0, keepdims=True)
    left[...] = gram + jnp.where(eye, 1e-05 * trace / width, 0.0)
    right[...] = jnp.where(eye, 1.0, 0.0)
    place = lax.broadcasted_iota(jnp.int32, (8, width), 0)
    contract = functools.partial(
        lax.dot_general,
        dimension_numbers=(((0,), (0,)), ((), ())),
        precision=lax.Precision.HIGHEST,
        preferred_element_type=jnp.float32,
    )

    def panel(step, carry):
        rows_left, rows_right = left[:8, :], right[:8, :]
        columns = [jnp.broadcast_to(rows_left[:, i : i + 1], (8, width)) for i in range(8)]
        done_left = jnp.zeros((8, width), jnp.float32)
        done_right = jnp.zeros((8, width), jnp.float32)
        for i in range(8):
            inverse = lax.rsqrt(columns[i][i : i + 1, :])
            top_left, top_right = rows_left[i : i + 1, :] * inverse, rows_right[i : i + 1, :] * inverse
            done_left = jnp.where(place == i, top_left, done_left)
            done_right = jnp.where(place == i, top_right, done_right)
            if i < 7:
                factor = jnp.where(place > i, columns[i] * inverse, 0.0)
                rows_left = rows_left - factor * top_left
                rows_right = rows_right - factor * top_right
                for j in range(i + 1, 8):
                    columns[j] = columns[j] - factor * (columns[j][i : i + 1, :] * inverse)
        out_ref[pl.ds(pl.multiple_of(step * 8, 8), 8), :] = done_right * scale
        new_left = pltpu.roll(left[...] - contract(done_left, done_left), width - 8, 1)
        new_right = right[...] - contract(done_left, done_right)
        left[: width - 8, :] = new_left[8:, :]
        right[: width - 8, :] = new_right[8:, :]
        left[width - 8 :, :] = jnp.zeros((8, width), jnp.float32)
        right[width - 8 :, :] = jnp.zeros((8, width), jnp.float32)
        return carry

    lax.fori_loop(0, width // 8, panel, 0)


def whitening(gram, count):
    shape = jax.ShapeDtypeStruct(gram.shape, jnp.float32)
    return pl.pallas_call(
        functools.partial(whiten_body, math.sqrt(count)),
        out_shape=shape,
        in_specs=[pl.BlockSpec(memory_space=pltpu.VMEM)],
        out_specs=pl.BlockSpec(memory_space=pltpu.VMEM),
        scratch_shapes=[pltpu.VMEM(gram.shape, jnp.float32)] * 2,
        compiler_params=pltpu.CompilerParams(vmem_limit_bytes=16 * 1024 * 1024),
    )(gram)


def transposed_product(left, right):
    return lax.dot_general(
        left, right, (((0,), (0,)), ((), ())), preferred_element_type=jnp.float32
    )


def as_rows(vector):
    length = vector.shape[0]
    padded = -(-length // 128) * 128
    return jnp.pad(vector, (0, padded - length)).reshape(padded // 128, 128)


def shards(counts, sketch):
    cell_dev, gene_dev = counts.shape
    n, m = lax.axis_size("cells"), lax.axis_size("genes")
    cell_count = float(cell_dev * n)
    gene_count = float(gene_dev * m)
    cell_part = jnp.sum(counts, axis=1).astype(jnp.float32)
    gene_part = jnp.sum(counts, axis=0).astype(jnp.float32)
    gene_rows, cell_rows, grand_rows = all_totals(as_rows(gene_part), as_rows(cell_part), n, m, 0)
    gene_total = gene_rows.reshape(-1)[:gene_dev]
    cell_total = cell_rows.reshape(-1)[:cell_dev]
    frac = gene_total / jnp.sum(grand_rows[0])
    limit = math.sqrt(cell_count)
    resid = residual_block(counts, cell_total, frac, limit)
    gene_scale = math.sqrt(gene_count) / cell_count
    omega = sketch
    basis = None
    for sweep in range(ITERS):
        ident = 1 + 4 * sweep
        part = jnp.dot(resid, omega, preferred_element_type=jnp.float32)
        own = scatter_genes(part, m, ident)
        gram = sum_gram(self_gram(own), n, m, ident + 1)
        own_basis = lax.dot_general(
            own,
            whitening(gram, cell_count),
            (((1,), (1,)), ((), ())),
            precision=lax.Precision.HIGHEST,
            preferred_element_type=jnp.float32,
        )
        basis = gather_genes(own_basis.astype(jnp.bfloat16), m, ident + 2)
        partial_sum = transposed_product(resid, basis)
        omega = loading_total(partial_sum, gene_scale, n, ident + 3)
    return (basis.astype(jnp.float32), omega.astype(jnp.float32))


def solution(mesh):
    return jax.shard_map(
        shards,
        mesh=mesh,
        in_specs=(P("cells", "genes"), P("genes", None)),
        out_specs=(P("cells", None), P("genes", None)),
        check_vma=False,
    )
```

profile of v0, /device:TPU:0, one launch (start us, length us, event | category | flops | bytes accessed | tf_op | source)
XLA Modules:
  0.0 200.2 jit_solution(11339043551644682157)
XLA Ops:
  0.6 0.0 copy-start
  0.6 8.2 %fusion.6 = (s32[4864]{0:T(1024)S(1)}, s32[1000]{0:T(1024)S(1)}) fusion(s32[4864,1000]{0,1:T(8,128)} %param.2), kind=kLoop, calls=%fused_computation.18 | loop fusion | flops 9722136 | bytes 19479456 | tf_op jit(solution)/shard_map/reduce_sum | solution.py:351
  8.8 11.8 %shard_map.41 = (f32[8,128]{1,0:T(8,128)S(1)}, f32[38,128]{1,0:T(8,128)S(1)}, f32[8,128]{1,0:T(8,128)S(1)}) custom-call(f32[8,128]{1,0:T(8,128)S(1)} %pad_bitcast_fusion.gene_ref, f32[38,128]{1,0:T(8,128)S(1)} %convert_bitcast_fusion.cell_ref), custom_call_target="tpu_custom_call" | custom-call | tf_op jit(solution)/shard_map/pallas_call | solution.py:49
  20.6 0.6 slice_reduce_fusion
  21.2 0.6 slice_divide_fusion
  21.9 10.2 %fusion.2 = bf16[4864,1000]{0,1:T(8,128)(2,1)S(1)} fusion(s32[4864,1000]{0,1:T(8,128)} %param.2, f32[1000]{0:T(1024)S(1)} %slice_divide_fusion, f32[4864]{0:T(1024)S(1)} %bitcast.46), kind=kLoop, calls=%fused_computation.6 | loop fusion | flops 43776000 | bytes 29207456 | tf_op jit(solution)/shard_map/convert_element_type | solution.py:265
  32.0 0.0 copy-done
  32.1 3.0 %fusion.7 = f32[4864,128]{1,0:T(8,128)S(1)} fusion(bf16[4864,1000]{0,1:T(8,128)(2,1)S(1)} %fusion.2, bf16[1000,128]{1,0:T(8,128)(2,1)S(1)} %copy-done), kind=kOutput, calls=%fused_computation.19 | convolution fusion | flops 1245184000 | bytes 12474368 | tf_op jit(solution)/shard_map/dot_general | solution.py:364
  35.1 18.5 %shard_map.42 = f32[1216,128]{1,0:T(8,128)S(1)} custom-call(f32[2,2,1216,128]{3,2,1,0:T(8,128)S(1)} %bitcast.35), custom_call_target="tpu_custom_call" | custom-call | tf_op jit(solution)/shard_map/pallas_call | solution.py:49
  53.6 1.2 fusion.8
  54.8 15.1 %shard_map.43 = f32[8,16,128]{2,1,0:T(8,128)S(1)} custom-call(f32[8,16,128]{2,1,0:T(8,128)S(1)} %bitcast.42), custom_call_target="tpu_custom_call" | custom-call | tf_op jit(solution)/shard_map/pallas_call | solution.py:49
  69.9 9.0 %shard_map.44 = f32[128,128]{1,0:T(8,128)S(1)} custom-call(f32[128,128]{1,0:T(8,128)S(1)} %bitcast.44), custom_call_target="tpu_custom_call" | custom-call | tf_op jit(solution)/shard_map/pallas_call | solution.py:324
  78.9 0.7 convolution_convert_fusion.1.x_ref
  79.6 10.9 %shard_map.45 = bf16[2,2,1216,128]{3,2,1,0:T(8,128)(2,1)S(1)} custom-call(bf16[1216,128]{1,0:T(8,128)(2,1)S(1)} %convolution_convert_fusion.1.x_ref), custom_call_target="tpu_custom_call" | custom-call | tf_op jit(solution)/shard_map/pallas_call | solution.py:49
  90.5 2.8 %fusion.9 = f32[1000,128]{1,0:T(8,128)S(1)} fusion(bf16[4864,1000]{0,1:T(8,128)(2,1)S(1)} %fusion.2, bf16[4864,128]{1,0:T(8,128)(2,1)S(1)} %bitcast.39), kind=kOutput, calls=%fused_computation.21 | convolution fusion | flops 1245184000 | bytes 11485184 | tf_op jit(solution)/shard_map/dot_general | solution.py:335
  93.3 21.8 %shard_map.46 = bf16[8,128,128]{2,1,0:T(8,128)(2,1)S(1)} custom-call(f32[8,128,128]{2,1,0:T(8,128)S(1)} %bitcast.38), custom_call_target="tpu_custom_call" | custom-call | tf_op jit(solution)/shard_map/pallas_call | solution.py:49
  115.1 3.0 %fusion.4 = f32[4864,128]{1,0:T(8,128)S(1)} fusion(bf16[4864,1000]{0,1:T(8,128)(2,1)S(1)} %fusion.2, bf16[1024,128]{1,0:T(8,128)(2,1)S(1)} %bitcast.41), kind=kOutput, calls=%fused_computation.11 | convolution fusion | flops 1245184000 | bytes 12474368 | tf_op jit(solution)/shard_map/dot_general | solution.py:364
  118.1 16.8 %shard_map.47 = f32[1216,128]{1,0:T(8,128)S(1)} custom-call(f32[2,2,1216,128]{3,2,1,0:T(8,128)S(1)} %bitcast.34), custom_call_target="tpu_custom_call" | custom-call | tf_op jit(solution)/shard_map/pallas_call | solution.py:49
  134.8 1.2 fusion.10
  136.1 15.4 %shard_map.48 = f32[8,16,128]{2,1,0:T(8,128)S(1)} custom-call(f32[8,16,128]{2,1,0:T(8,128)S(1)} %bitcast.43), custom_call_target="tpu_custom_call" | custom-call | tf_op jit(solution)/shard_map/pallas_call | solution.py:49
  151.5 8.8 %shard_map.49 = f32[128,128]{1,0:T(8,128)S(1)} custom-call(f32[128,128]{1,0:T(8,128)S(1)} %bitcast.45), custom_call_target="tpu_custom_call" | custom-call | tf_op jit(solution)/shard_map/pallas_call | solution.py:324
  160.3 0.7 convolution_convert_fusion.x_ref
  161.0 9.9 %shard_map.50 = bf16[2,2,1216,128]{3,2,1,0:T(8,128)(2,1)S(1)} custom-call(bf16[1216,128]{1,0:T(8,128)(2,1)S(1)} %convolution_convert_fusion.x_ref), custom_call_target="tpu_custom_call" | custom-call | tf_op jit(solution)/shard_map/pallas_call | solution.py:49
  170.9 2.8 %fusion.11 = f32[1000,128]{1,0:T(8,128)S(1)} fusion(bf16[4864,1000]{0,1:T(8,128)(2,1)S(1)} %fusion.2, bf16[4864,128]{1,0:T(8,128)(2,1)S(1)} %bitcast.36), kind=kOutput, calls=%fused_computation.23 | convolution fusion | flops 1245184000 | bytes 11485184 | tf_op jit(solution)/shard_map/dot_general | solution.py:335
  173.7 23.9 %shard_map.51 = bf16[8,128,128]{2,1,0:T(8,128)(2,1)S(1)} custom-call(f32[8,128,128]{2,1,0:T(8,128)S(1)} %bitcast.37), custom_call_target="tpu_custom_call" | custom-call | tf_op jit(solution)/shard_map/pallas_call | solution.py:49
  197.6 0.8 slice_convert_fusion
  198.5 1.7 bitcast_convert_fusion
  (5 shorter events, 0.1 us)
Async XLA Ops:
  0.6 31.4 %copy-start = (bf16[1000,128]{1,0:T(8,128)(2,1)S(1)}, bf16[1000,128]{1,0:T(8,128)(2,1)}, u32[]{:S(2)}) copy-start(bf16[1000,128]{1,0:T(8,128)(2,1)} %param.3) | copy-start | bytes 768004
where the time goes:
time: 200 us
  Pallas kernels  162 us (81%)
  other arithmetic  22.1 us (11%)
  matrix products  15.3 us (8%)
    pallas_call x9, Pallas kernels, call(): pl.pallas_call(body, out_shape=out_shape, in_specs=[pl.BlockSpec(memory_s...  144 us
    pallas_call x2, Pallas kernels, whitening(): pl.pallas_call(functools.partial(whiten_body, math.sqrt(count)), out_shap...  17.8 us
    convert_element_type x1, other arithmetic, residual_block(): return jnp.clip(scaled, -limit, limit).astype(jnp.bfloat16)  10.2 us
    reduce_sum x1, other arithmetic, shards(): cell_part = jnp.sum(counts, axis=1).astype(jnp.float32)  8.15 us
    dot_general x2, matrix products, shards(): part = jnp.dot(resid, omega, preferred_element_type=jnp.float32)  5.98 us
    dot_general x2, matrix products, transposed_product(): lax.dot_general(left, right, (((0,), (0,)), ((), ())), preferred_element_...  5.52 us

commit v1 on v0

v1 whole, which is shorter than its diff:
```python
import functools
import math

import jax
import jax.numpy as jnp
from jax import lax
from jax.experimental import pallas as pl
from jax.experimental.pallas import tpu as pltpu
from jax.sharding import PartitionSpec as P

ITERS = 2
CHUNK = 256
HALF = CHUNK // 2
BLOCK = 64
NEAR_LAG = 2
BASIS_LAG = 2
CODE = 32767.0
MIDDLE = 32768.0
MESH = pl.DeviceIdType.MESH


def ring_peers(axis, count):
    me = lax.axis_index(axis)
    return [{axis: lax.rem(me + step, count)} for step in range(1, count)]


def remote(src, dst, send_sem, recv_sem, peer):
    return pltpu.make_async_remote_copy(
        src_ref=src, dst_ref=dst, send_sem=send_sem, recv_sem=recv_sem, device_id=peer, device_id_type=MESH
    )


def encode(values):
    half = values.shape[0] // 2
    most = jnp.max(jnp.abs(values), axis=0, keepdims=True)
    inverse = jnp.where(most > 1e-30, CODE / most, 0.0)
    codes = (values * inverse + (MIDDLE + 0.5)).astype(jnp.int32)
    packed = codes[:half] | lax.shift_left(codes[half:], jnp.int32(16))
    return packed, most * (1.0 / CODE)


def decode(packed, unit):
    low = lax.bitwise_and(packed, jnp.int32(0xFFFF)).astype(jnp.float32)
    high = lax.shift_right_logical(packed, jnp.int32(16)).astype(jnp.float32)
    return jnp.concatenate([low - MIDDLE, high - MIDDLE], axis=0) * unit


def dot(left, right, left_dim, right_dim, precision=None):
    return lax.dot_general(
        left,
        right,
        (((left_dim,), (right_dim,)), ((), ())),
        precision=precision,
        preferred_element_type=jnp.float32,
    )


def split_terms(values):
    high = values.astype(jnp.bfloat16)
    return high, (values - high.astype(jnp.float32)).astype(jnp.bfloat16)


def whiten(gram, scale, out_ref, left, right):
    width = gram.shape[0]
    eye = lax.broadcasted_iota(jnp.int32, (width, width), 0) == lax.broadcasted_iota(jnp.int32, (width, width), 1)
    diagonal = jnp.where(eye, gram, 0.0)
    trace = jnp.sum(jnp.sum(diagonal, axis=1, keepdims=True), axis=0, keepdims=True)
    left[...] = gram + jnp.where(eye, 1e-05 * trace / width, 0.0)
    right[...] = jnp.where(eye, 1.0, 0.0)
    place = lax.broadcasted_iota(jnp.int32, (8, width), 0)

    def panel(step, carry):
        rows_left, rows_right = left[:8, :], right[:8, :]
        columns = [jnp.broadcast_to(rows_left[:, i : i + 1], (8, width)) for i in range(8)]
        done_left = jnp.zeros((8, width), jnp.float32)
        done_right = jnp.zeros((8, width), jnp.float32)
        for i in range(8):
            inverse = lax.rsqrt(columns[i][i : i + 1, :])
            top_left, top_right = rows_left[i : i + 1, :] * inverse, rows_right[i : i + 1, :] * inverse
            done_left = jnp.where(place == i, top_left, done_left)
            done_right = jnp.where(place == i, top_right, done_right)
            if i < 7:
                factor = jnp.where(place > i, columns[i] * inverse, 0.0)
                rows_left = rows_left - factor * top_left
                rows_right = rows_right - factor * top_right
                for j in range(i + 1, 8):
                    columns[j] = columns[j] - factor * (columns[j][i : i + 1, :] * inverse)
        out_ref[pl.ds(pl.multiple_of(step * 8, 8), 8), :] = done_right * scale
        new_left = pltpu.roll(left[...] - dot(done_left, done_left, 0, 0, lax.Precision.HIGHEST), width - 8, 1)
        new_right = right[...] - dot(done_left, done_right, 0, 0, lax.Precision.HIGHEST)
        left[: width - 8, :] = new_left[8:, :]
        right[: width - 8, :] = new_right[8:, :]
        left[width - 8 :, :] = jnp.zeros((8, width), jnp.float32)
        right[width - 8 :, :] = jnp.zeros((8, width), jnp.float32)
        return carry

    lax.fori_loop(0, width // 8, panel, 0)


def loop(count, body):
    lax.fori_loop(0, count, lambda i, carry: (body(i), carry)[1], 0)


def body(
    n,
    m,
    gene_dev,
    limit,
    gene_scale,
    counts_ref,
    sketch_ref,
    basis_ref,
    load_ref,
    counts,
    resid,
    gene_acc,
    frac,
    omega,
    part,
    near,
    codes,
    units,
    terms,
    product,
    gram_acc,
    gene_all,
    cell_all,
    grand_all,
    gram_all,
    gram_rows,
    gram_part,
    load_part,
    load_part_unit,
    load_all,
    load_unit,
    load_sum,
    load_sum_unit,
    left,
    right,
    white,
    in_sem,
    gene_sem,
    cell_sem,
    grand_sem,
    near_sem,
    code_sem,
    unit_sem,
    term_sem,
    gram_sem,
    rows_sem,
    piece_sem,
    piece_unit_sem,
    all_sem,
    all_unit_sem,
):
    f32, bf16 = jnp.float32, jnp.bfloat16
    chunks, rows8, _ = counts.shape
    padded = resid.shape[1]
    width = left.shape[0]
    gene_rows = padded // 128
    cells_me, genes_me = lax.axis_index("cells"), lax.axis_index("genes")
    y_count = m // 2
    core, row = lax.rem(genes_me, 2), lax.div(genes_me, 2)
    partner = {"genes": row * 2 + 1 - core}
    y_peers = [{"genes": lax.rem(row + step, y_count) * 2 + core} for step in range(1, y_count)]
    cell_peers = ring_peers("cells", n)
    gene_peers = ring_peers("genes", m)

    def fetch(i):
        start = pl.multiple_of(i * CHUNK, CHUNK)
        return pltpu.make_async_copy(counts_ref.at[:, pl.ds(start, CHUNK)], counts.at[i], in_sem.at[i])

    loop(chunks, lambda i: fetch(i).start())
    barrier = pltpu.get_barrier_semaphore()
    for peer in cell_peers + gene_peers:
        pl.semaphore_signal(barrier, inc=1, device_id=peer, device_id_type=MESH)
    gene_acc[...] = jnp.zeros(gene_acc.shape, jnp.int32)
    omega[...] = jnp.zeros(omega.shape, bf16)
    omega[:gene_dev, :] = sketch_ref[...]
    step_rows = max(k for k in range(8, 65, 8) if rows8 % k == 0)

    def total_chunk(i):
        fetch(i).wait()

        def add(k, total):
            start = pl.ds(pl.multiple_of(k * step_rows, 8), step_rows)
            block = counts[i, start, :]
            gene_acc[start, :] += block[:, :HALF] + block[:, HALF:]
            for r in range(0, step_rows, 8):
                total = total + block[r : r + 8, :]
            return total

        total = lax.fori_loop(0, rows8 // step_rows, add, jnp.zeros((8, CHUNK), jnp.int32))
        cell_all[genes_me, i] = jnp.sum(total, axis=0, keepdims=True).astype(f32)

    loop(chunks, total_chunk)
    for b in range(gene_rows):
        across = gene_acc[128 * b : 128 * (b + 1), :].astype(f32).T
        gene_all[cells_me, b] = jnp.sum(across, axis=0, keepdims=True)
    pl.semaphore_wait(barrier, len(cell_peers) + len(gene_peers))

    def share(buffer, place, sem, peers):
        copies = [
            remote(buffer.at[place], buffer.at[place], sem.at[0, i], sem.at[1, i], peer) for i, peer in enumerate(peers)
        ]
        for copy in copies:
            copy.start()
        return copies

    pending = []
    gene_copies = share(gene_all, cells_me, gene_sem, cell_peers)
    cell_copies = share(cell_all, genes_me, cell_sem, gene_peers)
    for copy in gene_copies:
        copy.wait_recv()
    gene_total = gene_all[0]
    for s in range(1, n):
        gene_total = gene_total + gene_all[s]
    grand = jnp.sum(jnp.sum(gene_total, axis=0), axis=1, keepdims=True)
    grand_all[genes_me] = jnp.broadcast_to(grand, (8, 128))
    grand_copies = share(grand_all, genes_me, grand_sem, gene_peers)
    for copy in grand_copies:
        copy.wait_recv()
    grand = grand_all[0]
    for s in range(1, m):
        grand = grand + grand_all[s]
    for b in range(gene_rows):
        share_row = jnp.where(gene_total[b] > 0.0, gene_total[b] / grand[:1], 1.0)
        frac[128 * b : 128 * (b + 1), :] = jnp.broadcast_to(share_row, (128, 128)).T
    for copy in cell_copies:
        copy.wait_recv()
    pending += gene_copies + cell_copies + grand_copies

    def residual(i):
        cell_total = cell_all[0, i]
        for s in range(1, m):
            cell_total = cell_total + cell_all[s, i]

        def block(start, real):
            values = counts[i, pl.ds(start, real), :].astype(f32)
            share_of = frac[pl.ds(start, real), :]
            expected = jnp.concatenate([share_of, share_of], axis=1) * cell_total
            scaled = (values - expected) * lax.rsqrt(expected + 0.01 * expected * expected)
            return jnp.clip(scaled, -limit, limit).astype(bf16)

        def full(k):
            start = pl.multiple_of(k * BLOCK, BLOCK)
            resid[i, pl.ds(start, BLOCK), :] = block(start, BLOCK)

        loop(rows8 // BLOCK, full)
        done = rows8 // BLOCK * BLOCK
        if rows8 > done:
            last = block(done, rows8 - done)
            resid[i, done : done + BLOCK, :] = jnp.concatenate(
                [last, jnp.zeros((done + BLOCK - rows8, CHUNK), bf16)], axis=0
            )
            done += BLOCK
        if padded > done:
            resid[i, done:, :] = jnp.zeros((padded - done, CHUNK), bf16)

    for sweep in range(ITERS):

        def near_copy(i):
            return remote(
                part.at[sweep, i, 1 - core],
                near.at[sweep, i],
                near_sem.at[sweep, 0, i],
                near_sem.at[sweep, 1, i],
                partner,
            )

        def code_copies(i):
            pairs = []
            for s, peer in enumerate(y_peers):
                for buffer, sem in ((codes, code_sem), (units, unit_sem)):
                    here = buffer.at[sweep, row, i]
                    pairs.append(remote(here, here, sem.at[sweep, 0, s, i], sem.at[sweep, 1, s, i], peer))
            return pairs

        def term_copy(i):
            here = terms.at[sweep, i, core]
            return remote(here, here, term_sem.at[sweep, 0, i], term_sem.at[sweep, 1, i], partner)

        def first(i):
            @pl.when(i < chunks)
            def _():
                if sweep == 0:
                    residual(i)
                rows = dot(resid[i], omega[...], 0, 0)
                part[sweep, i, 0] = rows[:HALF]
                part[sweep, i, 1] = rows[HALF:]
                near_copy(i).start()

            @pl.when(i >= NEAR_LAG)
            def _():
                j = i - NEAR_LAG
                near_copy(j).wait_recv()
                packed, unit = encode(part[sweep, j, core] + near[sweep, j])
                codes[sweep, row, j] = packed
                units[sweep, row, j] = unit
                for copy in code_copies(j):
                    copy.start()

        loop(chunks + NEAR_LAG, first)
        product[...] = jnp.zeros(product.shape, f32)
        gram_acc[...] = jnp.zeros(gram_acc.shape, f32)

        def second(i):
            @pl.when(i < chunks)
            def _():
                for copy in code_copies(i):
                    copy.wait_recv()
                total = decode(codes[sweep, 0, i], units[sweep, 0, i])
                for s in range(1, y_count):
                    total = total + decode(codes[sweep, s, i], units[sweep, s, i])
                high, low = split_terms(total)
                terms[sweep, i, core] = jnp.concatenate([high, low], axis=1)
                term_copy(i).start()

            @pl.when(i >= BASIS_LAG)
            def _():
                j = i - BASIS_LAG
                term_copy(j).wait_recv()
                both = terms[sweep, j].reshape(CHUNK, 2 * width)
                gram_acc[...] += dot(both, both, 0, 0)
                product[...] += dot(resid[j], both, 1, 0)

        loop(chunks + BASIS_LAG, second)

        gram = gram_acc[:width, :width] + gram_acc[:width, width:] + (gram_acc[width:, :width] + gram_acc[width:, width:])
        strip = width // m
        for g in range(m):
            gram_part[g] = gram[strip * g : strip * (g + 1)]
        gram_all[sweep, cells_me] = gram_part[genes_me]
        gram_copies = share(gram_all.at[sweep], cells_me, gram_sem.at[sweep], cell_peers)
        piece = padded // n
        for p in range(n):
            mine = product[piece * p : piece * (p + 1), :width] + product[piece * p : piece * (p + 1), width:]
            packed, unit = encode(mine)
            load_part[sweep, p] = packed
            load_part_unit[sweep, p] = unit
        piece_copies = []
        for s, peer in enumerate(cell_peers):
            for src, dst, sem in (
                (load_part, load_all, piece_sem),
                (load_part_unit, load_unit, piece_unit_sem),
            ):
                copy = remote(
                    src.at[sweep, peer["cells"]], dst.at[sweep, cells_me], sem.at[sweep, 0, s], sem.at[sweep, 1, s], peer
                )
                copy.start()
                piece_copies.append(copy)
        load_all[sweep, cells_me] = load_part[sweep, cells_me]
        load_unit[sweep, cells_me] = load_part_unit[sweep, cells_me]
        for copy in gram_copies:
            copy.wait_recv()
        total = gram_all[sweep, 0]
        for s in range(1, n):
            total = total + gram_all[sweep, s]
        gram_rows[sweep, genes_me] = total
        rows_copies = share(gram_rows.at[sweep], genes_me, rows_sem.at[sweep], gene_peers)
        for copy in piece_copies:
            copy.wait_recv()
        total = decode(load_all[sweep, 0], load_unit[sweep, 0])
        for s in range(1, n):
            total = total + decode(load_all[sweep, s], load_unit[sweep, s])
        packed, unit = encode(total)
        load_sum[sweep, cells_me] = packed
        load_sum_unit[sweep, cells_me] = unit
        all_copies = share(load_sum.at[sweep], cells_me, all_sem.at[sweep], cell_peers)
        all_copies += share(load_sum_unit.at[sweep], cells_me, all_unit_sem.at[sweep], cell_peers)
        for copy in rows_copies:
            copy.wait_recv()
        whiten(gram_rows[sweep].reshape(width, width), math.sqrt(chunks * CHUNK * n), white, left, right)
        last = sweep == ITERS - 1
        if last:
            high, low = split_terms(white[...].T)
            wide = jnp.concatenate([high, low], axis=1)
            wide = jnp.concatenate([wide, wide], axis=0)

            def write(i):
                rows = dot(terms[sweep, i].reshape(CHUNK, 2 * width), wide, 1, 0)
                start = pl.multiple_of(i * CHUNK, CHUNK)
                basis_ref[pl.ds(start, CHUNK), :] = rows[:, :width] + rows[:, width:]

            loop(chunks, write)
        for copy in all_copies:
            copy.wait_recv()
        scaled_white = white[...] * gene_scale
        for p in range(n):
            loads = dot(decode(load_sum[sweep, p], load_sum_unit[sweep, p]), scaled_white, 1, 1, lax.Precision.HIGHEST)
            start, stop = piece * p, min(piece * (p + 1), gene_dev)
            if last and stop > start:
                load_ref[start:stop, :] = loads[: stop - start]
            elif not last:
                omega[start : piece * (p + 1), :] = loads.astype(bf16)
        for copy in gram_copies + piece_copies + rows_copies + all_copies:
            copy.wait_send()

        def drain(i):
            near_copy(i).wait_send()
            for copy in code_copies(i):
                copy.wait_send()
            term_copy(i).wait_send()

        loop(chunks, drain)
    for copy in pending:
        copy.wait_send()


def shards(counts, sketch):
    cell_dev, gene_dev = counts.shape
    n, m = lax.axis_size("cells"), lax.axis_size("genes")
    width = sketch.shape[1]
    rows8 = -(-gene_dev // 8) * 8
    unit = max(16 * n, 128)
    padded = -(-gene_dev // unit) * unit
    chunks = cell_dev // CHUNK
    assert chunks * CHUNK == cell_dev and m % 2 == 0 and width % (8 * m) == 0
    table = counts.T
    if rows8 > gene_dev:
        table = jnp.pad(table, ((0, rows8 - gene_dev), (0, 0)))
    cell_count = float(cell_dev * n)
    gene_scale = math.sqrt(float(gene_dev * m)) / cell_count
    f32, bf16, i32 = jnp.float32, jnp.bfloat16, jnp.int32
    y_count = m // 2
    piece = padded // n
    vmem = pltpu.VMEM
    dma = pltpu.SemaphoreType.DMA
    scratch = [
        vmem((chunks, rows8, CHUNK), i32),
        vmem((chunks, padded, CHUNK), bf16),
        vmem((padded, 128), i32),
        vmem((padded, 128), f32),
        vmem((padded, width), bf16),
        vmem((ITERS, chunks, 2, HALF, width), f32),
        vmem((ITERS, chunks, HALF, width), f32),
        vmem((ITERS, y_count, chunks, HALF // 2, width), i32),
        vmem((ITERS, y_count, chunks, 1, width), f32),
        vmem((ITERS, chunks, 2, HALF, 2 * width), bf16),
        vmem((padded, 2 * width), f32),
        vmem((2 * width, 2 * width), f32),
        vmem((n, padded // 128, 1, 128), f32),
        vmem((m, chunks, 1, CHUNK), f32),
        vmem((m, 8, 128), f32),
        vmem((ITERS, n, width // m, width), f32),
        vmem((ITERS, m, width // m, width), f32),
        vmem((m, width // m, width), f32),
        vmem((ITERS, n, piece // 2, width), i32),
        vmem((ITERS, n, 1, width), f32),
        vmem((ITERS, n, piece // 2, width), i32),
        vmem((ITERS, n, 1, width), f32),
        vmem((ITERS, n, piece // 2, width), i32),
        vmem((ITERS, n, 1, width), f32),
        vmem((width, width), f32),
        vmem((width, width), f32),
        vmem((width, width), f32),
        dma((chunks,)),
        dma((2, n - 1)),
        dma((2, m - 1)),
        dma((2, m - 1)),
        dma((ITERS, 2, chunks)),
        dma((ITERS, 2, max(y_count - 1, 1), chunks)),
        dma((ITERS, 2, max(y_count - 1, 1), chunks)),
        dma((ITERS, 2, chunks)),
        dma((ITERS, 2, n - 1)),
        dma((ITERS, 2, m - 1)),
        dma((ITERS, 2, n - 1)),
        dma((ITERS, 2, n - 1)),
        dma((ITERS, 2, n - 1)),
        dma((ITERS, 2, n - 1)),
    ]
    basis, loadings = pl.pallas_call(
        functools.partial(body, n, m, gene_dev, math.sqrt(cell_count), gene_scale),
        out_shape=[jax.ShapeDtypeStruct((cell_dev, width), f32), jax.ShapeDtypeStruct((gene_dev, width), f32)],
        in_specs=[pl.BlockSpec(memory_space=pl.ANY), pl.BlockSpec(memory_space=pltpu.VMEM)],
        out_specs=[pl.BlockSpec(memory_space=pltpu.VMEM)] * 2,
        scratch_shapes=scratch,
        compiler_params=pltpu.CompilerParams(
            collective_id=0, has_side_effects=True, vmem_limit_bytes=58 * 1024 * 1024
        ),
    )(table, sketch)
    return basis, loadings


def solution(mesh):
    return jax.shard_map(
        shards,
        mesh=mesh,
        in_specs=(P("cells", "genes"), P("genes", None)),
        out_specs=(P("cells", None), P("genes", None)),
        check_vma=False,
    )
```

time: 200 us -> 120 us (0.60)
  Pallas kernels: 162 us -> 115 us
  other arithmetic: 22.1 us -> 0 us
  matrix products: 15.3 us -> 0 us
  local copies, waits for them, and re-layouts: 0.09 us -> 4.16 us
    pallas_call x11 -> x1, Pallas kernels: 162 us -> 115 us  [shards(): pl.pallas_call(functools.partial(body, n, m, gene_dev, math.sqrt(cell_cou...]
    dot_general x8 -> x0, matrix products: 15.3 us -> none  [the longest x2 5.98 us: shards(): part = jnp.dot(resid, omega, preferred_element_type=jnp.float32)]
    convert_element_type x5 -> x0, other arithmetic: 12.7 us -> none  [the longest x1 10.2 us: residual_block(): return jnp.clip(scaled, -limit, limit).astype(jnp.bfloat16)]
    reduce_sum x2 -> x0, other arithmetic: 8.75 us -> none  [the longest x1 8.15 us: shards(): cell_part = jnp.sum(counts, axis=1).astype(jnp.float32)]
    unnamed x2 -> x4, local copies, waits for them, and re-layouts: 0.01 us -> 4.16 us
where the time goes in v1:
time: 120 us
  Pallas kernels  115 us (96%)
  local copies, waits for them, and re-layouts  4.16 us (3%)
    pallas_call x1, Pallas kernels, shards(): pl.pallas_call(functools.partial(body, n, m, gene_dev, math.sqrt(cell_cou...  115 us
    unnamed x4, local copies, waits for them, and re-layouts  4.16 us

profile of v1, /device:TPU:0, one launch (start us, length us, event | category | flops | bytes accessed | tf_op | source)
XLA Modules:
  0.0 120.1 jit_solution(2468157684995956674)
XLA Ops:
  0.6 115.3 %shard_map.41 = (f32[4864,128]{1,0:T(8,128)}, f32[1000,128]{1,0:T(8,128)}) custom-call(s32[1000,4864]{1,0:T(8,128)} %bitcast.1, bf16[1000,128]{1,0:T(8,128)(2,1)} %sketch_ref.1), custom_call_target="tpu_custom_call" | custom-call | tf_op jit(solution)/shard_map/pallas_call | solution.py:472
  115.9 0.0 copy-start
  116.0 3.4 %copy.6 = f32[4864,128]{1,0:T(8,128)} copy(f32[4864,128]{1,0:T(8,128)} %get-tuple-element.4) | data formatting | bytes 4980736
  119.3 0.0 copy-done
  119.3 0.8 copy.7
Async XLA Ops:
  115.9 3.4 %copy-start = (f32[1000,128]{1,0:T(8,128)S(1)}, f32[1000,128]{1,0:T(8,128)}, u32[]{:S(2)}) copy-start(f32[1000,128]{1,0:T(8,128)} %get-tuple-element.5) | copy-start | bytes 1536004

commit v2 on v1

v2 whole, which is shorter than its diff:
```python
import functools
import math

import jax
import jax.numpy as jnp
from jax import lax
from jax.experimental import pallas as pl
from jax.experimental.pallas import tpu as pltpu
from jax.sharding import PartitionSpec as P

ITERS = 2
CHUNK = 256
HALF = CHUNK // 2
BLOCK = 64
DEPTH = 256
NEAR_LAG = 4
EARLY_PANELS = 4
BASIS_LAG = 4
CODE = 32767.0
MIDDLE = 32768.0
MESH = pl.DeviceIdType.MESH


def ring_peers(axis, count):
    me = lax.axis_index(axis)
    return [{axis: lax.rem(me + step, count)} for step in range(1, count)]


def remote(src, dst, send_sem, recv_sem, peer):
    return pltpu.make_async_remote_copy(
        src_ref=src, dst_ref=dst, send_sem=send_sem, recv_sem=recv_sem, device_id=peer, device_id_type=MESH
    )


def encode(values):
    half = values.shape[0] // 2
    most = jnp.max(jnp.abs(values), axis=0, keepdims=True)
    inverse = jnp.where(most > 1e-30, CODE / most, 0.0)
    codes = (values * inverse + (MIDDLE + 0.5)).astype(jnp.int32)
    packed = codes[:half] | lax.shift_left(codes[half:], jnp.int32(16))
    return packed, most * (1.0 / CODE)


def decode(packed, unit):
    low = lax.bitwise_and(packed, jnp.int32(0xFFFF)).astype(jnp.float32)
    high = lax.shift_right_logical(packed, jnp.int32(16)).astype(jnp.float32)
    return jnp.concatenate([low - MIDDLE, high - MIDDLE], axis=0) * unit


def dot(left, right, left_dim, right_dim, precision=None):
    return lax.dot_general(
        left,
        right,
        (((left_dim,), (right_dim,)), ((), ())),
        precision=precision,
        preferred_element_type=jnp.float32,
    )


def split_terms(values):
    high = values.astype(jnp.bfloat16)
    return high, (values - high.astype(jnp.float32)).astype(jnp.bfloat16)


def whiten_start(gram, left, right):
    width = gram.shape[0]
    eye = lax.broadcasted_iota(jnp.int32, (width, width), 0) == lax.broadcasted_iota(jnp.int32, (width, width), 1)
    diagonal = jnp.where(eye, gram, 0.0)
    trace = jnp.sum(jnp.sum(diagonal, axis=1, keepdims=True), axis=0, keepdims=True)
    left[...] = gram + jnp.where(eye, 1e-05 * trace / width, 0.0)
    right[...] = jnp.where(eye, 1.0, 0.0)


def whiten_panels(start, stop, scale, out_ref, left, right):
    width = left.shape[0]
    place = lax.broadcasted_iota(jnp.int32, (8, width), 0)

    def panel(step, carry):
        rows_left, rows_right = left[:8, :], right[:8, :]
        columns = [jnp.broadcast_to(rows_left[:, i : i + 1], (8, width)) for i in range(8)]
        done_left = jnp.zeros((8, width), jnp.float32)
        done_right = jnp.zeros((8, width), jnp.float32)
        for i in range(8):
            inverse = lax.rsqrt(columns[i][i : i + 1, :])
            top_left, top_right = rows_left[i : i + 1, :] * inverse, rows_right[i : i + 1, :] * inverse
            done_left = jnp.where(place == i, top_left, done_left)
            done_right = jnp.where(place == i, top_right, done_right)
            if i < 7:
                factor = jnp.where(place > i, columns[i] * inverse, 0.0)
                rows_left = rows_left - factor * top_left
                rows_right = rows_right - factor * top_right
                for j in range(i + 1, 8):
                    columns[j] = columns[j] - factor * (columns[j][i : i + 1, :] * inverse)
        out_ref[pl.ds(pl.multiple_of(step * 8, 8), 8), :] = done_right * scale
        new_left = pltpu.roll(left[...] - dot(done_left, done_left, 0, 0, lax.Precision.HIGHEST), width - 8, 1)
        new_right = right[...] - dot(done_left, done_right, 0, 0, lax.Precision.HIGHEST)
        left[: width - 8, :] = new_left[8:, :]
        right[: width - 8, :] = new_right[8:, :]
        left[width - 8 :, :] = jnp.zeros((8, width), jnp.float32)
        right[width - 8 :, :] = jnp.zeros((8, width), jnp.float32)
        return carry

    lax.fori_loop(start, stop, panel, 0)


def loop(count, body):
    lax.fori_loop(0, count, lambda i, carry: (body(i), carry)[1], 0)


def staged(count, lag, step):
    lag = min(lag, count)
    loop(lag, lambda i: step(i, True, False))
    lax.fori_loop(lag, count, lambda i, carry: (step(i, True, True), carry)[1], 0)
    lax.fori_loop(count, count + lag, lambda i, carry: (step(i, False, True), carry)[1], 0)


def body(
    n,
    m,
    gene_dev,
    limit,
    gene_scale,
    counts_ref,
    sketch_ref,
    basis_ref,
    load_ref,
    counts,
    resid,
    gene_acc,
    frac,
    omega,
    part,
    near,
    codes,
    units,
    terms,
    product,
    gram_acc,
    gene_all,
    cell_all,
    grand_all,
    gram_all,
    gram_rows,
    gram_part,
    load_part,
    load_part_unit,
    load_all,
    load_unit,
    load_sum,
    load_sum_unit,
    left,
    right,
    white,
    in_sem,
    gene_sem,
    cell_sem,
    grand_sem,
    near_sem,
    code_sem,
    unit_sem,
    term_sem,
    gram_sem,
    rows_sem,
    piece_sem,
    piece_unit_sem,
    all_sem,
    all_unit_sem,
):
    f32, bf16 = jnp.float32, jnp.bfloat16
    chunks, rows8, _ = counts.shape
    padded = resid.shape[1]
    width = left.shape[0]
    gene_rows = padded // 128
    cells_me, genes_me = lax.axis_index("cells"), lax.axis_index("genes")
    y_count = m // 2
    core, row = lax.rem(genes_me, 2), lax.div(genes_me, 2)
    partner = {"genes": row * 2 + 1 - core}
    y_peers = [{"genes": lax.rem(row + step, y_count) * 2 + core} for step in range(1, y_count)]
    cell_peers = ring_peers("cells", n)
    gene_peers = ring_peers("genes", m)

    def fetch(i):
        start = pl.multiple_of(i * CHUNK, CHUNK)
        return pltpu.make_async_copy(counts_ref.at[:, pl.ds(start, CHUNK)], counts.at[i], in_sem.at[i])

    loop(chunks, lambda i: fetch(i).start())
    sketch_copy = pltpu.make_async_copy(sketch_ref, omega.at[pl.ds(0, rows8)], in_sem.at[chunks])
    sketch_copy.start()
    barrier = pltpu.get_barrier_semaphore()

    def other(s):
        return {"cells": lax.rem(cells_me + lax.div(s, m), n), "genes": lax.rem(genes_me + lax.rem(s, m), m)}

    def greet(s):
        pl.semaphore_signal(barrier, inc=1, device_id=other(s + 1), device_id_type=MESH)

    loop(n * m - 1, greet)
    gene_acc[...] = jnp.zeros(gene_acc.shape, jnp.int32)
    if padded > rows8:
        omega[rows8:, :] = jnp.zeros((padded - rows8, width), bf16)
    step_rows = max(k for k in range(8, 65, 8) if rows8 % k == 0)

    def total_chunk(i):
        fetch(i).wait()

        def add(k, total):
            start = pl.ds(pl.multiple_of(k * step_rows, 8), step_rows)
            block = counts[i, start, :]
            gene_acc[start, :] += block[:, :HALF] + block[:, HALF:]
            for r in range(0, step_rows, 8):
                total = total + block[r : r + 8, :]
            return total

        total = lax.fori_loop(0, rows8 // step_rows, add, jnp.zeros((8, CHUNK), jnp.int32))
        cell_all[genes_me, i] = jnp.sum(total, axis=0, keepdims=True).astype(f32)

    with jax.named_scope("stream"):
        loop(chunks, total_chunk)
    for b in range(gene_rows):
        across = gene_acc[128 * b : 128 * (b + 1), :].astype(f32).T
        gene_row = jnp.sum(across, axis=0, keepdims=True)
        gene_all[cells_me, b] = gene_row
        grand = gene_row if b == 0 else grand + gene_row
    grand_all[cells_me * m + genes_me] = jnp.broadcast_to(jnp.sum(grand, axis=1, keepdims=True), (1, 128))
    with jax.named_scope("barrier"):
        pl.semaphore_wait(barrier, n * m - 1)

    def send_all(src, dst, sem, peers):
        for s, peer in enumerate(peers):
            remote(src(peer), dst, sem.at[0], sem.at[1], peer).start()

    def share(buffer, place, sem, peers):
        send_all(lambda peer: buffer.at[place], buffer.at[place], sem, peers)
        everything = buffer.at[pl.ds(0, len(peers))]
        return remote(everything, everything, sem.at[0], sem.at[1], peers[0])

    gene_copies = share(gene_all, cells_me, gene_sem, cell_peers)
    cell_copies = share(cell_all, genes_me, cell_sem, gene_peers)
    me = cells_me * m + genes_me

    def grand_start(s):
        here = grand_all.at[me]
        remote(here, here, grand_sem.at[0], grand_sem.at[1], other(s + 1)).start()

    loop(n * m - 1, grand_start)
    everything = grand_all.at[pl.ds(0, n * m - 1)]
    grand_copies = remote(everything, everything, grand_sem.at[0], grand_sem.at[1], other(1))
    with jax.named_scope("wait_gene"):
        gene_copies.wait_recv()
    gene_total = gene_all[0]
    for s in range(1, n):
        gene_total = gene_total + gene_all[s]
    with jax.named_scope("wait_grand"):
        grand_copies.wait_recv()
    grand = jnp.sum(grand_all[...], axis=0)
    for b in range(gene_rows):
        share_row = jnp.where(gene_total[b] > 0.0, gene_total[b] / grand, 1.0)
        frac[128 * b : 128 * (b + 1), :] = jnp.broadcast_to(share_row, (128, 128)).T
    with jax.named_scope("wait_cell"):
        cell_copies.wait_recv()

    def residual(i):
        cell_total = cell_all[0, i]
        for s in range(1, m):
            cell_total = cell_total + cell_all[s, i]
        sums = None
        for start in range(0, padded, DEPTH):
            stop = min(start + DEPTH, padded)
            blocks = []
            for k in range(start, min(stop, rows8), BLOCK):
                real = min(k + BLOCK, stop, rows8) - k
                share_of = frac[k : k + real, :]
                expected = jnp.concatenate([share_of, share_of], axis=1) * cell_total
                scaled = (counts[i, k : k + real, :].astype(f32) - expected) * lax.rsqrt(
                    expected + 0.01 * expected * expected
                )
                blocks.append(jnp.clip(scaled, -limit, limit))
            if stop > rows8:
                blocks.append(jnp.zeros((stop - max(start, rows8), CHUNK), f32))
            values = jnp.concatenate(blocks, axis=0).astype(bf16)
            resid[i, start:stop, :] = values
            term = dot(values, omega[start:stop, :], 0, 0)
            sums = term if sums is None else sums + term
        return sums

    sketch_copy.wait()
    for sweep in range(ITERS):

        def near_copy(i):
            return remote(part.at[i, 1 - core], near.at[sweep, i], near_sem.at[chunks], near_sem.at[i], partner)

        def code_start(i):
            for peer in y_peers:
                for buffer, sem in ((codes, code_sem), (units, unit_sem)):
                    here = buffer.at[sweep, row, i]
                    remote(here, here, sem.at[chunks], sem.at[i], peer).start()

        def code_wait(i):
            for buffer, sem in ((codes, code_sem), (units, unit_sem)):
                here = buffer.at[sweep, pl.ds(0, y_count - 1), i]
                remote(here, here, sem.at[chunks], sem.at[i], y_peers[0]).wait_recv()

        def term_copy(i):
            here = terms.at[sweep, i, core]
            return remote(here, here, term_sem.at[chunks], term_sem.at[i], partner)

        def first(i, sketch, code):
            j = i - NEAR_LAG
            if code:
                near_copy(j).wait_recv()
                packed, unit = encode(part[j, core] + near[sweep, j])
                codes[sweep, row, j] = packed
                units[sweep, row, j] = unit
            if sketch:
                rows = residual(i) if sweep == 0 else dot(resid[i], omega[...], 0, 0)
                part[i, 0] = rows[:HALF]
                part[i, 1] = rows[HALF:]
                near_copy(i).start()
            if code:
                code_start(j)

        def second(i, decoding, multiply):
            j = i - BASIS_LAG
            if decoding:
                code_wait(i)
            if multiply:
                term_copy(j).wait_recv()
                both = terms[sweep, j].reshape(CHUNK, 2 * width)
                gram_acc[...] += dot(both, both, 0, 0)
                product[...] += dot(resid[j], both, 1, 0)
            if decoding:
                total = decode(codes[sweep, 0, i], units[sweep, 0, i])
                for s in range(1, y_count):
                    total = total + decode(codes[sweep, s, i], units[sweep, s, i])
                high, low = split_terms(total)
                terms[sweep, i, core] = jnp.concatenate([high, low], axis=1)
                term_copy(i).start()

        with jax.named_scope(f"first{sweep}"):
            staged(chunks, NEAR_LAG, first)
        product[...] = jnp.zeros(product.shape, f32)
        gram_acc[...] = jnp.zeros(gram_acc.shape, f32)
        with jax.named_scope(f"second{sweep}"):
            staged(chunks, BASIS_LAG, second)

        gram = gram_acc[:width, :width] + gram_acc[:width, width:] + (gram_acc[width:, :width] + gram_acc[width:, width:])
        strip = width // m
        for g in range(m):
            gram_part[g] = gram[strip * g : strip * (g + 1)]
        gram_all[sweep, cells_me] = gram_part[genes_me]
        gram_copies = share(gram_all.at[sweep], cells_me, gram_sem, cell_peers)
        piece = padded // n
        for p in range(n):
            mine = product[piece * p : piece * (p + 1), :width] + product[piece * p : piece * (p + 1), width:]
            packed, unit = encode(mine)
            load_part[sweep, p] = packed
            load_part_unit[sweep, p] = unit
        piece_copies = []
        for src, dst, sem in ((load_part, load_all, piece_sem), (load_part_unit, load_unit, piece_unit_sem)):
            send_all(lambda peer: src.at[sweep, peer["cells"]], dst.at[sweep, cells_me], sem, cell_peers)
            most = pl.ds(0, n - 1)
            piece_copies.append(
                remote(src.at[sweep, most], dst.at[sweep, most], sem.at[0], sem.at[1], cell_peers[0])
            )
        load_all[sweep, cells_me] = load_part[sweep, cells_me]
        load_unit[sweep, cells_me] = load_part_unit[sweep, cells_me]
        with jax.named_scope(f"wait_gram{sweep}"):
            gram_copies.wait_recv()
        total = gram_all[sweep, 0]
        for s in range(1, n):
            total = total + gram_all[sweep, s]
        gram_rows[sweep, genes_me] = total
        rows_copies = share(gram_rows.at[sweep], genes_me, rows_sem, gene_peers)
        with jax.named_scope(f"wait_rows{sweep}"):
            rows_copies.wait_recv()
        panels = width // 8
        early = min(EARLY_PANELS, panels)
        scale = math.sqrt(chunks * CHUNK * n)
        with jax.named_scope(f"whiten{sweep}"):
            whiten_start(gram_rows[sweep].reshape(width, width), left, right)
            whiten_panels(0, early, scale, white, left, right)
        with jax.named_scope(f"wait_piece{sweep}"):
            for copy in piece_copies:
                copy.wait_recv()
        total = decode(load_all[sweep, 0], load_unit[sweep, 0])
        for s in range(1, n):
            total = total + decode(load_all[sweep, s], load_unit[sweep, s])
        packed, unit = encode(total)
        load_sum[sweep, cells_me] = packed
        load_sum_unit[sweep, cells_me] = unit
        all_copies = share(load_sum.at[sweep], cells_me, all_sem, cell_peers)
        all_unit_copies = share(load_sum_unit.at[sweep], cells_me, all_unit_sem, cell_peers)
        with jax.named_scope(f"whiten{sweep}"):
            whiten_panels(early, panels, scale, white, left, right)
        last = sweep == ITERS - 1
        if last:
            high, low = split_terms(white[...].T)
            wide = jnp.concatenate([high, low], axis=1)
            wide = jnp.concatenate([wide, wide], axis=0)

            def write(i):
                rows = dot(terms[sweep, i].reshape(CHUNK, 2 * width), wide, 1, 0)
                start = pl.multiple_of(i * CHUNK, CHUNK)
                basis_ref[pl.ds(start, CHUNK), :] = rows[:, :width] + rows[:, width:]

            with jax.named_scope("write"):
                lax.fori_loop(0, chunks, lambda i, carry: (write(i), carry)[1], 0, unroll=True)
        with jax.named_scope(f"wait_all{sweep}"):
            all_copies.wait_recv()
            all_unit_copies.wait_recv()
        scaled_white = white[...] * gene_scale
        for p in range(n):
            loads = dot(decode(load_sum[sweep, p], load_sum_unit[sweep, p]), scaled_white, 1, 1, lax.Precision.HIGHEST)
            start, stop = piece * p, min(piece * (p + 1), gene_dev)
            if last and stop > start:
                load_ref[start:stop, :] = loads[: stop - start]
            elif not last:
                omega[start : piece * (p + 1), :] = loads.astype(bf16)
        for copies in [gram_copies, rows_copies, all_copies, all_unit_copies] + piece_copies:
            copies.wait_send()
        near_all, term_all = near.at[sweep], terms.at[sweep, pl.ds(0, chunks), core]
        remote(near_all, near_all, near_sem.at[chunks], near_sem.at[0], partner).wait_send()
        remote(term_all, term_all, term_sem.at[chunks], term_sem.at[0], partner).wait_send()
        for buffer, sem in ((codes, code_sem), (units, unit_sem)):
            here = buffer.at[sweep, pl.ds(0, y_count - 1)]
            remote(here, here, sem.at[chunks], sem.at[0], y_peers[0]).wait_send()
    for copies in (gene_copies, cell_copies, grand_copies):
        copies.wait_send()


def shards(counts, sketch):
    cell_dev, gene_dev = counts.shape
    n, m = lax.axis_size("cells"), lax.axis_size("genes")
    width = sketch.shape[1]
    rows8 = -(-gene_dev // 8) * 8
    unit = max(16 * n, 128)
    padded = -(-gene_dev // unit) * unit
    chunks = cell_dev // CHUNK
    assert chunks * CHUNK == cell_dev and m % 2 == 0 and width % (8 * m) == 0
    table = counts.T
    if rows8 > gene_dev:
        table = jnp.pad(table, ((0, rows8 - gene_dev), (0, 0)))
        sketch = jnp.pad(sketch, ((0, rows8 - gene_dev), (0, 0)))
    cell_count = float(cell_dev * n)
    gene_scale = math.sqrt(float(gene_dev * m)) / cell_count
    f32, bf16, i32 = jnp.float32, jnp.bfloat16, jnp.int32
    y_count = m // 2
    piece = padded // n
    vmem = pltpu.VMEM
    dma = pltpu.SemaphoreType.DMA
    scratch = [
        vmem((chunks, rows8, CHUNK), i32),
        vmem((chunks, padded, CHUNK), bf16),
        vmem((padded, 128), i32),
        vmem((padded, 128), f32),
        vmem((padded, width), bf16),
        vmem((chunks, 2, HALF, width), f32),
        vmem((ITERS, chunks, HALF, width), f32),
        vmem((ITERS, y_count, chunks, HALF // 2, width), i32),
        vmem((ITERS, y_count, chunks, 1, width), f32),
        vmem((ITERS, chunks, 2, HALF, 2 * width), bf16),
        vmem((padded, 2 * width), f32),
        vmem((2 * width, 2 * width), f32),
        vmem((n, padded // 128, 1, 128), f32),
        vmem((m, chunks, 1, CHUNK), f32),
        vmem((n * m, 1, 128), f32),
        vmem((ITERS, n, width // m, width), f32),
        vmem((ITERS, m, width // m, width), f32),
        vmem((m, width // m, width), f32),
        vmem((ITERS, n, piece // 2, width), i32),
        vmem((ITERS, n, 1, width), f32),
        vmem((ITERS, n, piece // 2, width), i32),
        vmem((ITERS, n, 1, width), f32),
        vmem((ITERS, n, piece // 2, width), i32),
        vmem((ITERS, n, 1, width), f32),
        vmem((width, width), f32),
        vmem((width, width), f32),
        vmem((width, width), f32),
        dma((chunks + 1,)),
        dma((2,)),
        dma((2,)),
        dma((2,)),
        dma((chunks + 1,)),
        dma((chunks + 1,)),
        dma((chunks + 1,)),
        dma((chunks + 1,)),
        dma((2,)),
        dma((2,)),
        dma((2,)),
        dma((2,)),
        dma((2,)),
        dma((2,)),
    ]
    basis, loadings = pl.pallas_call(
        functools.partial(body, n, m, gene_dev, math.sqrt(cell_count), gene_scale),
        out_shape=[jax.ShapeDtypeStruct((cell_dev, width), f32), jax.ShapeDtypeStruct((gene_dev, width), f32)],
        in_specs=[pl.BlockSpec(memory_space=pltpu.HBM)] * 2,
        out_specs=[pl.BlockSpec(memory_space=pltpu.VMEM)] * 2,
        scratch_shapes=scratch,
        compiler_params=pltpu.CompilerParams(
            collective_id=0, has_side_effects=True, vmem_limit_bytes=50 * 1024 * 1024
        ),
    )(table, sketch)
    return basis, loadings


def solution(mesh):
    return jax.shard_map(
        shards,
        mesh=mesh,
        in_specs=(P("cells", "genes"), P("genes", None)),
        out_specs=(P("cells", None), P("genes", None)),
        check_vma=False,
    )
```

time: 120 us -> 103 us (0.86)
  Pallas kernels: 115 us -> 98.8 us
    pallas_call x1, Pallas kernels: 115 us -> 98.8 us  [shards(): pl.pallas_call(functools.partial(body, n, m, gene_dev, math.sqrt(cell_cou...]
where the time goes in v2:
time: 103 us
  Pallas kernels  98.8 us (96%)
  local copies, waits for them, and re-layouts  3.18 us (3%)
    pallas_call x1, Pallas kernels, shards(): pl.pallas_call(functools.partial(body, n, m, gene_dev, math.sqrt(cell_cou...  98.8 us
    unnamed x4, local copies, waits for them, and re-layouts  3.18 us

profile of v2, /device:TPU:0, one launch (start us, length us, event | category | flops | bytes accessed | tf_op | source)
XLA Modules:
  0.0 102.6 jit_solution(17752074478249205516)
XLA Ops:
  0.6 0.0 copy-start
  0.6 0.9 copy-done
  1.6 98.8 %shard_map.41 = (f32[4864,128]{1,0:T(8,128)S(1)}, f32[1000,128]{1,0:T(8,128)S(1)}) custom-call(s32[1000,4864]{1,0:T(8,128)} %bitcast.1, bf16[1000,128]{1,0:T(8,128)(2,1)S(1)} %copy-done), custom_call_target="tpu_custom_call" | custom-call | tf_op jit(solution)/shard_map/pallas_call | solution.py:494
  100.4 1.5 %copy.6 = f32[4864,128]{1,0:T(8,128)} copy(f32[4864,128]{1,0:T(8,128)S(1)} %get-tuple-element.4) | data formatting | bytes 4980736
  101.9 0.8 copy.7
Async XLA Ops:
  0.6 0.9 copy-start

commit v3 on v2

--- a/solution.py
+++ b/solution.py
@@ -14,16 +14,18 @@
 BLOCK = 64
 DEPTH = 256
 NEAR_LAG = 4
-EARLY_PANELS = 4
+FIRST_PIECES = 5
 BASIS_LAG = 4
 CODE = 32767.0
 MIDDLE = 32768.0
 MESH = pl.DeviceIdType.MESH
 
 
-def ring_peers(axis, count):
-    me = lax.axis_index(axis)
-    return [{axis: lax.rem(me + step, count)} for step in range(1, count)]
+def far_first(count):
+    order = []
+    for i in range((count + 1) // 2):
+        order += [i] if 2 * i == count - 1 else [i, count - 1 - i]
+    return order
 
 
 def remote(src, dst, send_sem, recv_sem, peer):
@@ -75,32 +77,43 @@
     width = left.shape[0]
     place = lax.broadcasted_iota(jnp.int32, (8, width), 0)
 
-    def panel(step, carry):
-        rows_left, rows_right = left[:8, :], right[:8, :]
-        columns = [jnp.broadcast_to(rows_left[:, i : i + 1], (8, width)) for i in range(8)]
-        done_left = jnp.zeros((8, width), jnp.float32)
+    def spread(rows, step):
+        return [jnp.broadcast_to(rows[:, 8 * step + i : 8 * step + i + 1], (8, width)) for i in range(8)]
+
+    for step in range(start, stop):
+        here = slice(8 * step, 8 * step + 8)
+        rows_left, rows_right = left[here, :], right[here, :]
+        columns = spread(rows_left, step)
+        inverses, tops_left, tops_right, pivots = [], [], [], []
         done_right = jnp.zeros((8, width), jnp.float32)
         for i in range(8):
             inverse = lax.rsqrt(columns[i][i : i + 1, :])
             top_left, top_right = rows_left[i : i + 1, :] * inverse, rows_right[i : i + 1, :] * inverse
-            done_left = jnp.where(place == i, top_left, done_left)
             done_right = jnp.where(place == i, top_right, done_right)
-            if i < 7:
-                factor = jnp.where(place > i, columns[i] * inverse, 0.0)
-                rows_left = rows_left - factor * top_left
-                rows_right = rows_right - factor * top_right
+            factor = jnp.where(place > i, columns[i] * inverse, 0.0)
+            rows_left = rows_left - factor * top_left
+            rows_right = rows_right - factor * top_right
+            pivot = {}
+            for j in range(i + 1, 8):
+                pivot[j] = columns[j][i : i + 1, :] * inverse
+                columns[j] = columns[j] - factor * pivot[j]
+            inverses.append(inverse)
+            tops_left.append(top_left)
+            tops_right.append(top_right)
+            pivots.append(pivot)
+        out_ref[here, :] = done_right * scale
+        for block in range(step + 1, width // 8):
+            there = slice(8 * block, 8 * block + 8)
+            rows_left, rows_right = left[there, :], right[there, :]
+            columns = spread(rows_left, step)
+            for i in range(8):
+                factor = columns[i] * inverses[i]
+                rows_left = rows_left - factor * tops_left[i]
+                rows_right = rows_right - factor * tops_right[i]
                 for j in range(i + 1, 8):
-                    columns[j] = columns[j] - factor * (columns[j][i : i + 1, :] * inverse)
-        out_ref[pl.ds(pl.multiple_of(step * 8, 8), 8), :] = done_right * scale
-        new_left = pltpu.roll(left[...] - dot(done_left, done_left, 0, 0, lax.Precision.HIGHEST), width - 8, 1)
-        new_right = right[...] - dot(done_left, done_right, 0, 0, lax.Precision.HIGHEST)
-        left[: width - 8, :] = new_left[8:, :]
-        right[: width - 8, :] = new_right[8:, :]
-        left[width - 8 :, :] = jnp.zeros((8, width), jnp.float32)
-        right[width - 8 :, :] = jnp.zeros((8, width), jnp.float32)
-        return carry
-
-    lax.fori_loop(start, stop, panel, 0)
+                    columns[j] = columns[j] - factor * pivots[i][j]
+            left[there, :] = rows_left
+            right[there, :] = rows_right
 
 
 def loop(count, body):
@@ -142,6 +155,7 @@
     gram_all,
     gram_rows,
     gram_part,
+    gram_pair,
     load_part,
     load_part_unit,
     load_all,
@@ -159,6 +173,7 @@
     code_sem,
     unit_sem,
     term_sem,
+    pair_sem,
     gram_sem,
     rows_sem,
     piece_sem,
@@ -176,8 +191,9 @@
     core, row = lax.rem(genes_me, 2), lax.div(genes_me, 2)
     partner = {"genes": row * 2 + 1 - core}
     y_peers = [{"genes": lax.rem(row + step, y_count) * 2 + core} for step in range(1, y_count)]
-    cell_peers = ring_peers("cells", n)
-    gene_peers = ring_peers("genes", m)
+    beside = {"cells": lax.rem(cells_me + 1, n)}
+    parity, level = lax.rem(cells_me, 2), lax.div(cells_me, 2)
+    pair = {"cells": 2 * level + 1 - parity}
 
     def fetch(i):
         start = pl.multiple_of(i * CHUNK, CHUNK)
@@ -225,17 +241,20 @@
     with jax.named_scope("barrier"):
         pl.semaphore_wait(barrier, n * m - 1)
 
-    def send_all(src, dst, sem, peers):
-        for s, peer in enumerate(peers):
-            remote(src(peer), dst, sem.at[0], sem.at[1], peer).start()
-
-    def share(buffer, place, sem, peers):
-        send_all(lambda peer: buffer.at[place], buffer.at[place], sem, peers)
-        everything = buffer.at[pl.ds(0, len(peers))]
-        return remote(everything, everything, sem.at[0], sem.at[1], peers[0])
-
-    gene_copies = share(gene_all, cells_me, gene_sem, cell_peers)
-    cell_copies = share(cell_all, genes_me, cell_sem, gene_peers)
+    def share(buffer, axis, me, sem):
+        here = buffer.at[me]
+        count = lax.axis_size(axis)
+        for p in far_first(count):
+
+            @pl.when(p != me)
+            def _():
+                remote(here, here, sem.at[0], sem.at[1], {axis: p}).start()
+
+        everything = buffer.at[pl.ds(0, count - 1)]
+        return remote(everything, everything, sem.at[0], sem.at[1], {axis: lax.rem(me + 1, count)})
+
+    gene_copies = share(gene_all, "cells", cells_me, gene_sem)
+    cell_copies = share(cell_all, "genes", genes_me, cell_sem)
     me = cells_me * m + genes_me
 
     def grand_start(s):
@@ -344,41 +363,60 @@
             staged(chunks, BASIS_LAG, second)
 
         gram = gram_acc[:width, :width] + gram_acc[:width, width:] + (gram_acc[width:, :width] + gram_acc[width:, width:])
-        strip = width // m
-        for g in range(m):
-            gram_part[g] = gram[strip * g : strip * (g + 1)]
-        gram_all[sweep, cells_me] = gram_part[genes_me]
-        gram_copies = share(gram_all.at[sweep], cells_me, gram_sem, cell_peers)
+        gram_part[...] = gram.reshape(gram_part.shape)
+        pair_copy = remote(
+            gram_part.at[genes_me, 1 - parity], gram_pair.at[sweep], pair_sem.at[0], pair_sem.at[1], pair
+        )
+        pair_copy.start()
         piece = padded // n
-        for p in range(n):
-            mine = product[piece * p : piece * (p + 1), :width] + product[piece * p : piece * (p + 1), width:]
-            packed, unit = encode(mine)
+        piece_copies = []
+        def level_sum():
+            pair_copy.wait()
+            gram_all[sweep, level] = gram_part[genes_me, parity] + gram_pair[sweep]
+            for p in far_first(n // 2):
+                here = gram_all.at[sweep, level]
+
+                @pl.when(p != level)
+                def _():
+                    remote(here, here, gram_sem.at[0], gram_sem.at[1], {"cells": 2 * p + parity}).start()
+
+            everything = gram_all.at[sweep, pl.ds(0, n // 2 - 1)]
+            gram_copies = remote(everything, everything, gram_sem.at[0], gram_sem.at[1], beside)
+            return gram_copies
+
+        for step, p in enumerate(far_first(n)):
+            if step == min(FIRST_PIECES, n - 1):
+                gram_copies = level_sum()
+            rows = product[p * piece : (p + 1) * piece, :]
+            packed, unit = encode(rows[:, :width] + rows[:, width:])
             load_part[sweep, p] = packed
             load_part_unit[sweep, p] = unit
-        piece_copies = []
-        for src, dst, sem in ((load_part, load_all, piece_sem), (load_part_unit, load_unit, piece_unit_sem)):
-            send_all(lambda peer: src.at[sweep, peer["cells"]], dst.at[sweep, cells_me], sem, cell_peers)
-            most = pl.ds(0, n - 1)
-            piece_copies.append(
-                remote(src.at[sweep, most], dst.at[sweep, most], sem.at[0], sem.at[1], cell_peers[0])
-            )
+
+            @pl.when(p != cells_me)
+            def _():
+                for src, dst, sem in ((load_part, load_all, piece_sem), (load_part_unit, load_unit, piece_unit_sem)):
+                    remote(src.at[sweep, p], dst.at[sweep, cells_me], sem.at[0], sem.at[1], {"cells": p}).start()
+
         load_all[sweep, cells_me] = load_part[sweep, cells_me]
         load_unit[sweep, cells_me] = load_part_unit[sweep, cells_me]
+        for src, dst, sem in ((load_part, load_all, piece_sem), (load_part_unit, load_unit, piece_unit_sem)):
+            most = pl.ds(0, n - 1)
+            piece_copies.append(remote(src.at[sweep, most], dst.at[sweep, most], sem.at[0], sem.at[1], beside))
         with jax.named_scope(f"wait_gram{sweep}"):
             gram_copies.wait_recv()
         total = gram_all[sweep, 0]
-        for s in range(1, n):
+        for s in range(1, n // 2):
             total = total + gram_all[sweep, s]
-        gram_rows[sweep, genes_me] = total
-        rows_copies = share(gram_rows.at[sweep], genes_me, rows_sem, gene_peers)
-        with jax.named_scope(f"wait_rows{sweep}"):
-            rows_copies.wait_recv()
-        panels = width // 8
-        early = min(EARLY_PANELS, panels)
-        scale = math.sqrt(chunks * CHUNK * n)
-        with jax.named_scope(f"whiten{sweep}"):
-            whiten_start(gram_rows[sweep].reshape(width, width), left, right)
-            whiten_panels(0, early, scale, white, left, right)
+        mine = 2 * genes_me + parity
+        gram_rows[sweep, mine] = total
+        here = gram_rows.at[sweep, mine]
+        for step in range(1, 2 * m):
+            peer = {"genes": lax.rem(genes_me + step // 2, m)}
+            if step % 2:
+                peer["cells"] = pair["cells"]
+            remote(here, here, rows_sem.at[0], rows_sem.at[1], peer).start()
+        everything = gram_rows.at[sweep, pl.ds(0, 2 * m - 1)]
+        rows_copies = remote(everything, everything, rows_sem.at[0], rows_sem.at[1], beside)
         with jax.named_scope(f"wait_piece{sweep}"):
             for copy in piece_copies:
                 copy.wait_recv()
@@ -388,15 +426,19 @@
         packed, unit = encode(total)
         load_sum[sweep, cells_me] = packed
         load_sum_unit[sweep, cells_me] = unit
-        all_copies = share(load_sum.at[sweep], cells_me, all_sem, cell_peers)
-        all_unit_copies = share(load_sum_unit.at[sweep], cells_me, all_unit_sem, cell_peers)
+        all_copies = share(load_sum.at[sweep], "cells", cells_me, all_sem)
+        all_unit_copies = share(load_sum_unit.at[sweep], "cells", cells_me, all_unit_sem)
+        with jax.named_scope(f"wait_rows{sweep}"):
+            rows_copies.wait_recv()
+        scale = math.sqrt(chunks * CHUNK * n)
         with jax.named_scope(f"whiten{sweep}"):
-            whiten_panels(early, panels, scale, white, left, right)
+            whiten_start(gram_rows[sweep].reshape(width, width), left, right)
+            whiten_panels(0, width // 8, scale, white, left, right)
         last = sweep == ITERS - 1
+        high, low = split_terms(white[...].T)
+        wide = jnp.concatenate([high, low], axis=1)
+        wide = jnp.concatenate([wide, wide], axis=0)
         if last:
-            high, low = split_terms(white[...].T)
-            wide = jnp.concatenate([high, low], axis=1)
-            wide = jnp.concatenate([wide, wide], axis=0)
 
             def write(i):
                 rows = dot(terms[sweep, i].reshape(CHUNK, 2 * width), wide, 1, 0)
@@ -408,14 +450,16 @@
         with jax.named_scope(f"wait_all{sweep}"):
             all_copies.wait_recv()
             all_unit_copies.wait_recv()
-        scaled_white = white[...] * gene_scale
-        for p in range(n):
-            loads = dot(decode(load_sum[sweep, p], load_sum_unit[sweep, p]), scaled_white, 1, 1, lax.Precision.HIGHEST)
-            start, stop = piece * p, min(piece * (p + 1), gene_dev)
-            if last and stop > start:
-                load_ref[start:stop, :] = loads[: stop - start]
-            elif not last:
-                omega[start : piece * (p + 1), :] = loads.astype(bf16)
+        with jax.named_scope(f"loads{sweep}"):
+            for p in range(n):
+                high, low = split_terms(decode(load_sum[sweep, p], load_sum_unit[sweep, p]))
+                loads = dot(jnp.concatenate([high, low], axis=1), wide, 1, 0)
+                loads = (loads[:, :width] + loads[:, width:]) * gene_scale
+                start, stop = piece * p, min(piece * (p + 1), gene_dev)
+                if last and stop > start:
+                    load_ref[start:stop, :] = loads[: stop - start]
+                elif not last:
+                    omega[start : piece * (p + 1), :] = loads.astype(bf16)
         for copies in [gram_copies, rows_copies, all_copies, all_unit_copies] + piece_copies:
             copies.wait_send()
         near_all, term_all = near.at[sweep], terms.at[sweep, pl.ds(0, chunks), core]
@@ -436,7 +480,8 @@
     unit = max(16 * n, 128)
     padded = -(-gene_dev // unit) * unit
     chunks = cell_dev // CHUNK
-    assert chunks * CHUNK == cell_dev and m % 2 == 0 and width % (8 * m) == 0
+    strip = width // (2 * m)
+    assert chunks * CHUNK == cell_dev and m % 2 == 0 and n % 2 == 0 and strip % 8 == 0
     table = counts.T
     if rows8 > gene_dev:
         table = jnp.pad(table, ((0, rows8 - gene_dev), (0, 0)))
@@ -464,9 +509,10 @@
         vmem((n, padded // 128, 1, 128), f32),
         vmem((m, chunks, 1, CHUNK), f32),
         vmem((n * m, 1, 128), f32),
-        vmem((ITERS, n, width // m, width), f32),
-        vmem((ITERS, m, width // m, width), f32),
-        vmem((m, width // m, width), f32),
+        vmem((ITERS, n // 2, strip, width), f32),
+        vmem((ITERS, 2 * m, strip, width), f32),
+        vmem((m, 2, strip, width), f32),
+        vmem((ITERS, strip, width), f32),
         vmem((ITERS, n, piece // 2, width), i32),
         vmem((ITERS, n, 1, width), f32),
         vmem((ITERS, n, piece // 2, width), i32),
@@ -484,6 +530,7 @@
         dma((chunks + 1,)),
         dma((chunks + 1,)),
         dma((chunks + 1,)),
+        dma((2,)),
         dma((2,)),
         dma((2,)),
         dma((2,)),

time: 103 us -> 92.7 us (0.900)
  Pallas kernels: 98.8 us -> 88.7 us
    pallas_call x1, Pallas kernels: 98.8 us -> 88.7 us  [shards(): pl.pallas_call(functools.partial(body, n, m, gene_dev, math.sqrt(cell_cou...]
where the time goes in v3:
time: 92.7 us; the launch traced here: 92.5 us
  Pallas kernels  88.7 us (96%)
  local copies, waits for them, and re-layouts  3.18 us (3%)
    pallas_call x1, Pallas kernels, shards(): pl.pallas_call(functools.partial(body, n, m, gene_dev, math.sqrt(cell_cou...  88.7 us
    unnamed x4, local copies, waits for them, and re-layouts  3.18 us

profile of v3, /device:TPU:0, one launch (start us, length us, event | category | flops | bytes accessed | tf_op | source)
XLA Modules:
  0.0 92.5 jit_solution(1906243152884772957)
XLA Ops:
  0.6 0.0 copy-start
  0.6 0.9 %copy-done = bf16[1000,128]{1,0:T(8,128)(2,1)S(1)} copy-done((bf16[1000,128]{1,0:T(8,128)(2,1)S(1)}, bf16[1000,128]{1,0:T(8,128)(2,1)}, u32[]{:S(2)}) %copy-start) | copy-done | bytes 256024
  1.6 88.7 %shard_map.41 = (f32[4864,128]{1,0:T(8,128)S(1)}, f32[1000,128]{1,0:T(8,128)S(1)}) custom-call(s32[1000,4864]{1,0:T(8,128)} %bitcast.1, bf16[1000,128]{1,0:T(8,128)(2,1)S(1)} %copy-done), custom_call_target="tpu_custom_call" | custom-call | tf_op jit(solution)/shard_map/pallas_call | solution.py:541
  90.3 1.5 %copy.6 = f32[4864,128]{1,0:T(8,128)} copy(f32[4864,128]{1,0:T(8,128)S(1)} %get-tuple-element.4) | data formatting | bytes 4980736
  91.7 0.8 copy.7
Async XLA Ops:
  0.6 0.9 %copy-start = (bf16[1000,128]{1,0:T(8,128)(2,1)S(1)}, bf16[1000,128]{1,0:T(8,128)(2,1)}, u32[]{:S(2)}) copy-start(bf16[1000,128]{1,0:T(8,128)(2,1)} %sketch_ref.1) | copy-start | bytes 768004

commit v4 on v3

--- a/solution.py
+++ b/solution.py
@@ -12,8 +12,9 @@
 CHUNK = 256
 HALF = CHUNK // 2
 BLOCK = 64
-DEPTH = 256
+DEPTH = 128
 NEAR_LAG = 4
+GROUP = 5
 FIRST_PIECES = 5
 BASIS_LAG = 4
 CODE = 32767.0
@@ -80,11 +81,13 @@
     def spread(rows, step):
         return [jnp.broadcast_to(rows[:, 8 * step + i : 8 * step + i + 1], (8, width)) for i in range(8)]
 
+    ahead = []
     for step in range(start, stop):
         here = slice(8 * step, 8 * step + 8)
         rows_left, rows_right = left[here, :], right[here, :]
-        columns = spread(rows_left, step)
+        columns = ahead if ahead else spread(rows_left, step)
         inverses, tops_left, tops_right, pivots = [], [], [], []
+        ahead = []
         done_right = jnp.zeros((8, width), jnp.float32)
         for i in range(8):
             inverse = lax.rsqrt(columns[i][i : i + 1, :])
@@ -106,8 +109,12 @@
             there = slice(8 * block, 8 * block + 8)
             rows_left, rows_right = left[there, :], right[there, :]
             columns = spread(rows_left, step)
+            if block == step + 1:
+                ahead = spread(rows_left, block)
             for i in range(8):
                 factor = columns[i] * inverses[i]
+                if block == step + 1:
+                    ahead = [ahead[j] - factor * factor[j : j + 1, :] for j in range(8)]
                 rows_left = rows_left - factor * tops_left[i]
                 rows_right = rows_right - factor * tops_right[i]
                 for j in range(i + 1, 8):
@@ -125,6 +132,42 @@
     loop(lag, lambda i: step(i, True, False))
     lax.fori_loop(lag, count, lambda i, carry: (step(i, True, True), carry)[1], 0)
     lax.fori_loop(count, count + lag, lambda i, carry: (step(i, False, True), carry)[1], 0)
+
+
+def two_term_loads(packed, unit, wide):
+    high, low = split_terms(decode(packed, unit))
+    loads = dot(jnp.concatenate([high, low], axis=1), wide, 1, 0)
+    half = loads.shape[1] // 2
+    return loads[:, :half] + loads[:, half:]
+
+
+def write_body(
+    gene_dev, gene_scale, terms, wide_ref, sums, units, basis_out, load_out, basis, loadings, basis_sem, load_sem
+):
+    chunks = terms.shape[0]
+    width = basis.shape[1]
+    wide = wide_ref[...]
+    parts, members, part_rows, _ = sums.shape
+    copies = []
+    for p in range(members):
+        for q in range(parts):
+            start = 2 * part_rows * (p * parts + q)
+            stop = min(start + 2 * part_rows, gene_dev)
+            if stop > start:
+                loads = two_term_loads(sums[q, p], units[q, p], wide) * gene_scale
+                loadings[start:stop, :] = loads[: stop - start]
+    copies.append(pltpu.make_async_copy(loadings, load_out, load_sem))
+    copies[0].start()
+    for k, start in enumerate(range(0, chunks, GROUP)):
+        stop = min(start + GROUP, chunks)
+        for i in range(start, stop):
+            rows = dot(terms[i].reshape(CHUNK, 2 * width), wide, 1, 0)
+            basis[i * CHUNK : (i + 1) * CHUNK, :] = rows[:, :width] + rows[:, width:]
+        rows = pl.ds(start * CHUNK, (stop - start) * CHUNK)
+        copies.append(pltpu.make_async_copy(basis.at[rows], basis_out.at[rows], basis_sem.at[k]))
+        copies[-1].start()
+    for copy in copies:
+        copy.wait()
 
 
 def body(
@@ -135,8 +178,10 @@
     gene_scale,
     counts_ref,
     sketch_ref,
-    basis_ref,
-    load_ref,
+    last_terms,
+    wide_ref,
+    last_sum,
+    last_unit,
     counts,
     resid,
     gene_acc,
@@ -146,7 +191,7 @@
     near,
     codes,
     units,
-    terms,
+    first_terms,
     product,
     gram_acc,
     gene_all,
@@ -160,8 +205,10 @@
     load_part_unit,
     load_all,
     load_unit,
-    load_sum,
-    load_sum_unit,
+    swap,
+    swap_unit,
+    first_sum,
+    first_unit,
     left,
     right,
     white,
@@ -178,11 +225,14 @@
     rows_sem,
     piece_sem,
     piece_unit_sem,
+    swap_sem,
+    swap_unit_sem,
     all_sem,
     all_unit_sem,
 ):
     f32, bf16 = jnp.float32, jnp.bfloat16
     chunks, rows8, _ = counts.shape
+    parts = load_all.shape[1]
     padded = resid.shape[1]
     width = left.shape[0]
     gene_rows = padded // 128
@@ -278,6 +328,8 @@
     with jax.named_scope("wait_cell"):
         cell_copies.wait_recv()
 
+    low_limit, high_limit = jnp.asarray(-limit, bf16), jnp.asarray(limit, bf16)
+
     def residual(i):
         cell_total = cell_all[0, i]
         for s in range(1, m):
@@ -293,10 +345,10 @@
                 scaled = (counts[i, k : k + real, :].astype(f32) - expected) * lax.rsqrt(
                     expected + 0.01 * expected * expected
                 )
-                blocks.append(jnp.clip(scaled, -limit, limit))
+                blocks.append(scaled)
             if stop > rows8:
                 blocks.append(jnp.zeros((stop - max(start, rows8), CHUNK), f32))
-            values = jnp.concatenate(blocks, axis=0).astype(bf16)
+            values = jnp.clip(jnp.concatenate(blocks, axis=0).astype(bf16), low_limit, high_limit)
             resid[i, start:stop, :] = values
             term = dot(values, omega[start:stop, :], 0, 0)
             sums = term if sums is None else sums + term
@@ -304,6 +356,9 @@
 
     sketch_copy.wait()
     for sweep in range(ITERS):
+        last = sweep == ITERS - 1
+        terms = last_terms if last else first_terms
+        load_sum, load_sum_unit = (last_sum, last_unit) if last else (first_sum, first_unit)
 
         def near_copy(i):
             return remote(part.at[i, 1 - core], near.at[sweep, i], near_sem.at[chunks], near_sem.at[i], partner)
@@ -320,7 +375,7 @@
                 remote(here, here, sem.at[chunks], sem.at[i], y_peers[0]).wait_recv()
 
         def term_copy(i):
-            here = terms.at[sweep, i, core]
+            here = terms.at[i, core]
             return remote(here, here, term_sem.at[chunks], term_sem.at[i], partner)
 
         def first(i, sketch, code):
@@ -344,7 +399,7 @@
                 code_wait(i)
             if multiply:
                 term_copy(j).wait_recv()
-                both = terms[sweep, j].reshape(CHUNK, 2 * width)
+                both = terms[j].reshape(CHUNK, 2 * width)
                 gram_acc[...] += dot(both, both, 0, 0)
                 product[...] += dot(resid[j], both, 1, 0)
             if decoding:
@@ -352,7 +407,7 @@
                 for s in range(1, y_count):
                     total = total + decode(codes[sweep, s, i], units[sweep, s, i])
                 high, low = split_terms(total)
-                terms[sweep, i, core] = jnp.concatenate([high, low], axis=1)
+                terms[i, core] = jnp.concatenate([high, low], axis=1)
                 term_copy(i).start()
 
         with jax.named_scope(f"first{sweep}"):
@@ -365,11 +420,83 @@
         gram = gram_acc[:width, :width] + gram_acc[:width, width:] + (gram_acc[width:, :width] + gram_acc[width:, width:])
         gram_part[...] = gram.reshape(gram_part.shape)
         pair_copy = remote(
-            gram_part.at[genes_me, 1 - parity], gram_pair.at[sweep], pair_sem.at[0], pair_sem.at[1], pair
+            gram_part.at[genes_me, 1 - parity], gram_pair.at[sweep], pair_sem.at[sweep, 0], pair_sem.at[sweep, 1], pair
         )
         pair_copy.start()
-        piece = padded // n
-        piece_copies = []
+        members = n // 2
+        piece = padded // members
+        part_rows = piece // 2 // parts
+        side, member = lax.div(cells_me, members), lax.rem(cells_me, members)
+        across = {"cells": (1 - side) * members + member}
+        stage_sems = ((load_all, piece_sem), (load_unit, piece_unit_sem))
+
+        def scatter(q):
+            for p in range(members):
+                start = p * piece + q * 2 * part_rows
+                rows = product[start : start + 2 * part_rows, :]
+                packed, unit = encode(rows[:, :width] + rows[:, width:])
+                load_part[sweep, q, p] = packed
+                load_part_unit[sweep, q, p] = unit
+
+                @pl.when(p != member)
+                def _():
+                    for src, (dst, sem) in zip((load_part, load_part_unit), stage_sems):
+                        sems = sem.at[q, 0], sem.at[q, 1]
+                        remote(
+                            src.at[sweep, q, p], dst.at[sweep, q, member], *sems, {"cells": side * members + p}
+                        ).start()
+
+            load_all[sweep, q, member] = load_part[sweep, q, member]
+            load_unit[sweep, q, member] = load_part_unit[sweep, q, member]
+
+        def most_of(buffer, sem):
+            most = buffer.at[pl.ds(0, members - 1)]
+            return remote(most, most, sem.at[0], sem.at[1], across)
+
+        piece_copies = [
+            most_of(dst.at[sweep, q], sem.at[q]) for q in range(parts) for dst, sem in stage_sems
+        ]
+
+        def swap_copies(q):
+            return [
+                remote(buffer.at[sweep, q, side], buffer.at[sweep, q, side], sem.at[sweep, q, 0], sem.at[sweep, q, 1], across)
+                for buffer, sem in ((swap, swap_sem), (swap_unit, swap_unit_sem))
+            ]
+
+        def cross(q):
+            with jax.named_scope(f"wait_piece{q}{sweep}"):
+                piece_copies[2 * q].wait_recv()
+                piece_copies[2 * q + 1].wait_recv()
+            total = decode(load_all[sweep, q, 0], load_unit[sweep, q, 0])
+            for s in range(1, members):
+                total = total + decode(load_all[sweep, q, s], load_unit[sweep, q, s])
+            packed, unit = encode(total)
+            swap[sweep, q, side] = packed
+            swap_unit[sweep, q, side] = unit
+            for copy in swap_copies(q):
+                copy.start()
+
+        all_copies = []
+
+        def gather(q):
+            with jax.named_scope(f"wait_swap{q}{sweep}"):
+                for copy in swap_copies(q):
+                    copy.wait_recv()
+            total = decode(swap[sweep, q, 0], swap_unit[sweep, q, 0])
+            total = total + decode(swap[sweep, q, 1], swap_unit[sweep, q, 1])
+            packed, unit = encode(total)
+            load_sum[q, member] = packed
+            load_sum_unit[q, member] = unit
+            for buffer, sem in ((load_sum, all_sem), (load_sum_unit, all_unit_sem)):
+                here = buffer.at[q, member]
+                for p in range(members):
+
+                    @pl.when(p != member)
+                    def _():
+                        remote(here, here, sem.at[q, 0], sem.at[q, 1], {"cells": side * members + p}).start()
+
+                all_copies.append(most_of(buffer.at[q], sem.at[q]))
+
         def level_sum():
             pair_copy.wait()
             gram_all[sweep, level] = gram_part[genes_me, parity] + gram_pair[sweep]
@@ -378,30 +505,17 @@
 
                 @pl.when(p != level)
                 def _():
-                    remote(here, here, gram_sem.at[0], gram_sem.at[1], {"cells": 2 * p + parity}).start()
+                    remote(here, here, gram_sem.at[sweep, 0], gram_sem.at[sweep, 1], {"cells": 2 * p + parity}).start()
 
             everything = gram_all.at[sweep, pl.ds(0, n // 2 - 1)]
-            gram_copies = remote(everything, everything, gram_sem.at[0], gram_sem.at[1], beside)
+            gram_copies = remote(everything, everything, gram_sem.at[sweep, 0], gram_sem.at[sweep, 1], beside)
             return gram_copies
 
-        for step, p in enumerate(far_first(n)):
-            if step == min(FIRST_PIECES, n - 1):
-                gram_copies = level_sum()
-            rows = product[p * piece : (p + 1) * piece, :]
-            packed, unit = encode(rows[:, :width] + rows[:, width:])
-            load_part[sweep, p] = packed
-            load_part_unit[sweep, p] = unit
-
-            @pl.when(p != cells_me)
-            def _():
-                for src, dst, sem in ((load_part, load_all, piece_sem), (load_part_unit, load_unit, piece_unit_sem)):
-                    remote(src.at[sweep, p], dst.at[sweep, cells_me], sem.at[0], sem.at[1], {"cells": p}).start()
-
-        load_all[sweep, cells_me] = load_part[sweep, cells_me]
-        load_unit[sweep, cells_me] = load_part_unit[sweep, cells_me]
-        for src, dst, sem in ((load_part, load_all, piece_sem), (load_part_unit, load_unit, piece_unit_sem)):
-            most = pl.ds(0, n - 1)
-            piece_copies.append(remote(src.at[sweep, most], dst.at[sweep, most], sem.at[0], sem.at[1], beside))
+        for q in range(parts):
+            scatter(q)
+        gram_copies = level_sum()
+        for q in range(parts):
+            cross(q)
         with jax.named_scope(f"wait_gram{sweep}"):
             gram_copies.wait_recv()
         total = gram_all[sweep, 0]
@@ -414,55 +528,34 @@
             peer = {"genes": lax.rem(genes_me + step // 2, m)}
             if step % 2:
                 peer["cells"] = pair["cells"]
-            remote(here, here, rows_sem.at[0], rows_sem.at[1], peer).start()
+            remote(here, here, rows_sem.at[sweep, 0], rows_sem.at[sweep, 1], peer).start()
         everything = gram_rows.at[sweep, pl.ds(0, 2 * m - 1)]
-        rows_copies = remote(everything, everything, rows_sem.at[0], rows_sem.at[1], beside)
-        with jax.named_scope(f"wait_piece{sweep}"):
-            for copy in piece_copies:
-                copy.wait_recv()
-        total = decode(load_all[sweep, 0], load_unit[sweep, 0])
-        for s in range(1, n):
-            total = total + decode(load_all[sweep, s], load_unit[sweep, s])
-        packed, unit = encode(total)
-        load_sum[sweep, cells_me] = packed
-        load_sum_unit[sweep, cells_me] = unit
-        all_copies = share(load_sum.at[sweep], "cells", cells_me, all_sem)
-        all_unit_copies = share(load_sum_unit.at[sweep], "cells", cells_me, all_unit_sem)
+        rows_copies = remote(everything, everything, rows_sem.at[sweep, 0], rows_sem.at[sweep, 1], beside)
+        for q in range(parts):
+            gather(q)
         with jax.named_scope(f"wait_rows{sweep}"):
             rows_copies.wait_recv()
         scale = math.sqrt(chunks * CHUNK * n)
         with jax.named_scope(f"whiten{sweep}"):
             whiten_start(gram_rows[sweep].reshape(width, width), left, right)
             whiten_panels(0, width // 8, scale, white, left, right)
-        last = sweep == ITERS - 1
         high, low = split_terms(white[...].T)
         wide = jnp.concatenate([high, low], axis=1)
         wide = jnp.concatenate([wide, wide], axis=0)
         if last:
-
-            def write(i):
-                rows = dot(terms[sweep, i].reshape(CHUNK, 2 * width), wide, 1, 0)
-                start = pl.multiple_of(i * CHUNK, CHUNK)
-                basis_ref[pl.ds(start, CHUNK), :] = rows[:, :width] + rows[:, width:]
-
-            with jax.named_scope("write"):
-                lax.fori_loop(0, chunks, lambda i, carry: (write(i), carry)[1], 0, unroll=True)
+            wide_ref[...] = wide
         with jax.named_scope(f"wait_all{sweep}"):
-            all_copies.wait_recv()
-            all_unit_copies.wait_recv()
-        with jax.named_scope(f"loads{sweep}"):
-            for p in range(n):
-                high, low = split_terms(decode(load_sum[sweep, p], load_sum_unit[sweep, p]))
-                loads = dot(jnp.concatenate([high, low], axis=1), wide, 1, 0)
-                loads = (loads[:, :width] + loads[:, width:]) * gene_scale
-                start, stop = piece * p, min(piece * (p + 1), gene_dev)
-                if last and stop > start:
-                    load_ref[start:stop, :] = loads[: stop - start]
-                elif not last:
-                    omega[start : piece * (p + 1), :] = loads.astype(bf16)
-        for copies in [gram_copies, rows_copies, all_copies, all_unit_copies] + piece_copies:
+            for copies in all_copies:
+                copies.wait_recv()
+        if not last:
+            for p in range(members):
+                for q in range(parts):
+                    loads = two_term_loads(load_sum[q, p], load_sum_unit[q, p], wide)
+                    start = piece * p + 2 * part_rows * q
+                    omega[start : start + 2 * part_rows, :] = (loads * gene_scale).astype(bf16)
+        for copies in [gram_copies, rows_copies] + all_copies + piece_copies + swap_copies(0) + swap_copies(parts - 1)[: 2 * (parts - 1)]:
             copies.wait_send()
-        near_all, term_all = near.at[sweep], terms.at[sweep, pl.ds(0, chunks), core]
+        near_all, term_all = near.at[sweep], terms.at[pl.ds(0, chunks), core]
         remote(near_all, near_all, near_sem.at[chunks], near_sem.at[0], partner).wait_send()
         remote(term_all, term_all, term_sem.at[chunks], term_sem.at[0], partner).wait_send()
         for buffer, sem in ((codes, code_sem), (units, unit_sem)):
@@ -490,7 +583,10 @@
     gene_scale = math.sqrt(float(gene_dev * m)) / cell_count
     f32, bf16, i32 = jnp.float32, jnp.bfloat16, jnp.int32
     y_count = m // 2
-    piece = padded // n
+    members = n // 2
+    piece = padded // members
+    parts = 2 if piece % 32 == 0 else 1
+    part_rows = piece // 2 // parts
     vmem = pltpu.VMEM
     dma = pltpu.SemaphoreType.DMA
     scratch = [
@@ -503,7 +599,7 @@
         vmem((ITERS, chunks, HALF, width), f32),
         vmem((ITERS, y_count, chunks, HALF // 2, width), i32),
         vmem((ITERS, y_count, chunks, 1, width), f32),
-        vmem((ITERS, chunks, 2, HALF, 2 * width), bf16),
+        vmem((chunks, 2, HALF, 2 * width), bf16),
         vmem((padded, 2 * width), f32),
         vmem((2 * width, 2 * width), f32),
         vmem((n, padded // 128, 1, 128), f32),
@@ -513,12 +609,14 @@
         vmem((ITERS, 2 * m, strip, width), f32),
         vmem((m, 2, strip, width), f32),
         vmem((ITERS, strip, width), f32),
-        vmem((ITERS, n, piece // 2, width), i32),
-        vmem((ITERS, n, 1, width), f32),
-        vmem((ITERS, n, piece // 2, width), i32),
-        vmem((ITERS, n, 1, width), f32),
-        vmem((ITERS, n, piece // 2, width), i32),
-        vmem((ITERS, n, 1, width), f32),
+        vmem((ITERS, parts, members, part_rows, width), i32),
+        vmem((ITERS, parts, members, 1, width), f32),
+        vmem((ITERS, parts, members, part_rows, width), i32),
+        vmem((ITERS, parts, members, 1, width), f32),
+        vmem((ITERS, parts, 2, part_rows, width), i32),
+        vmem((ITERS, parts, 2, 1, width), f32),
+        vmem((parts, members, part_rows, width), i32),
+        vmem((parts, members, 1, width), f32),
         vmem((width, width), f32),
         vmem((width, width), f32),
         vmem((width, width), f32),
@@ -530,25 +628,45 @@
         dma((chunks + 1,)),
         dma((chunks + 1,)),
         dma((chunks + 1,)),
-        dma((2,)),
-        dma((2,)),
-        dma((2,)),
-        dma((2,)),
-        dma((2,)),
-        dma((2,)),
-        dma((2,)),
+        dma((ITERS, 2)),
+        dma((ITERS, 2)),
+        dma((ITERS, 2)),
+        dma((parts, 2)),
+        dma((parts, 2)),
+        dma((ITERS, parts, 2)),
+        dma((ITERS, parts, 2)),
+        dma((parts, 2)),
+        dma((parts, 2)),
     ]
-    basis, loadings = pl.pallas_call(
+    handed = [
+        jax.ShapeDtypeStruct((chunks, 2, HALF, 2 * width), bf16),
+        jax.ShapeDtypeStruct((2 * width, 2 * width), bf16),
+        jax.ShapeDtypeStruct((parts, members, part_rows, width), i32),
+        jax.ShapeDtypeStruct((parts, members, 1, width), f32),
+    ]
+    handed = pl.pallas_call(
         functools.partial(body, n, m, gene_dev, math.sqrt(cell_count), gene_scale),
-        out_shape=[jax.ShapeDtypeStruct((cell_dev, width), f32), jax.ShapeDtypeStruct((gene_dev, width), f32)],
+        out_shape=handed,
         in_specs=[pl.BlockSpec(memory_space=pltpu.HBM)] * 2,
-        out_specs=[pl.BlockSpec(memory_space=pltpu.VMEM)] * 2,
+        out_specs=[pl.BlockSpec(memory_space=pltpu.VMEM)] * 4,
         scratch_shapes=scratch,
         compiler_params=pltpu.CompilerParams(
-            collective_id=0, has_side_effects=True, vmem_limit_bytes=50 * 1024 * 1024
+            collective_id=0, has_side_effects=True, vmem_limit_bytes=48 * 1024 * 1024
         ),
     )(table, sketch)
-    return basis, loadings
+    return pl.pallas_call(
+        functools.partial(write_body, gene_dev, gene_scale),
+        out_shape=[jax.ShapeDtypeStruct((cell_dev, width), f32), jax.ShapeDtypeStruct((gene_dev, width), f32)],
+        in_specs=[pl.BlockSpec(memory_space=pltpu.VMEM)] * 4,
+        out_specs=[pl.BlockSpec(memory_space=pltpu.HBM)] * 2,
+        scratch_shapes=[
+            vmem((cell_dev, width), f32),
+            vmem((gene_dev, width), f32),
+            dma((-(-chunks // GROUP),)),
+            dma(()),
+        ],
+        compiler_params=pltpu.CompilerParams(vmem_limit_bytes=16 * 1024 * 1024),
+    )(*handed)
 
 
 def solution(mesh):

time: 92.7 us -> 89.2 us (0.962)
  local copies, waits for them, and re-layouts: 3.18 us -> 0.94 us
  Pallas kernels: 88.7 us -> 87.3 us
    pallas_call x1, Pallas kernels: 88.7 us -> 85.2 us  [shards(): pl.pallas_call(functools.partial(body, n, m, gene_dev, math.sqrt(cell_cou...]
    unnamed x4 -> x2, local copies, waits for them, and re-layouts: 3.18 us -> 0.94 us
    pallas_call x0 -> x1, Pallas kernels: none -> 2.14 us  [shards(): pl.pallas_call(functools.partial(write_body, gene_dev, gene_scale), out_s...]
where the time goes in v4:
time: 89.2 us; the launch traced here: 89 us
  Pallas kernels  87.3 us (98%)
  local copies, waits for them, and re-layouts  0.94 us (1%)
    pallas_call x1, Pallas kernels, shards(): pl.pallas_call(functools.partial(body, n, m, gene_dev, math.sqrt(cell_cou...  85.2 us
    pallas_call x1, Pallas kernels, shards(): pl.pallas_call(functools.partial(write_body, gene_dev, gene_scale), out_s...  2.14 us

profile of v4, /device:TPU:0, one launch (start us, length us, event | category | flops | bytes accessed | tf_op | source)
XLA Modules:
  0.0 89.0 jit_solution(14223434972009003817)
XLA Ops:
  0.6 0.0 copy-start
  0.6 0.9 %copy-done = bf16[1000,128]{1,0:T(8,128)(2,1)S(1)} copy-done((bf16[1000,128]{1,0:T(8,128)(2,1)S(1)}, bf16[1000,128]{1,0:T(8,128)(2,1)}, u32[]{:S(2)}) %copy-start) | copy-done | bytes 256024
  1.6 85.2 %shard_map.41 = (bf16[19,2,128,256]{3,2,1,0:T(8,128)(2,1)S(1)}, bf16[256,256]{1,0:T(8,128)(2,1)S(1)}, s32[2,4,64,128]{3,2,1,0:T(8,128)S(1)}, f32[2,4,1,128]{3,2,1,0:T(1,128)S(1)}) custom-call(s32[1000,4864]{1,0:T(8,128)} %bitcast.1, bf16[1000,128]{1,0:T(8,128)(2,1)S(1)} %copy-done), custom_call_target="tpu_custom_call" | custom-call | tf_op jit(solution)/shard_map/pallas_call | solution.py:647
  86.7 2.1 %shard_map.42 = (f32[4864,128]{1,0:T(8,128)}, f32[1000,128]{1,0:T(8,128)}) custom-call(bf16[19,2,128,256]{3,2,1,0:T(8,128)(2,1)S(1)} %get-tuple-element.6.terms, bf16[256,256]{1,0:T(8,128)(2,1)S(1)} %get-tuple-element.7.wide_ref, s32[2,4,64,128]{3,2,1,0:T(8,128)S(1)} %get-tuple-element.8.sums, f32[2,4,1,128]{3,2,1,0:T(1,128)S(1)} %get-tuple-element.9.units), custom_call_target="tpu_custom_call" | custom-call | tf_op jit(solution)/shard_map/pallas_call | solution.py:657
Async XLA Ops:
  0.6 0.9 %copy-start = (bf16[1000,128]{1,0:T(8,128)(2,1)S(1)}, bf16[1000,128]{1,0:T(8,128)(2,1)}, u32[]{:S(2)}) copy-start(bf16[1000,128]{1,0:T(8,128)(2,1)} %sketch_ref.1) | copy-start | bytes 768004

commit v5 on v4

--- a/solution.py
+++ b/solution.py
@@ -14,7 +14,7 @@
 BLOCK = 64
 DEPTH = 128
 NEAR_LAG = 4
-GROUP = 5
+GROUP = 4
 FIRST_PIECES = 5
 BASIS_LAG = 4
 CODE = 32767.0
@@ -149,6 +149,14 @@
     wide = wide_ref[...]
     parts, members, part_rows, _ = sums.shape
     copies = []
+    for k, start in enumerate(range(0, chunks, GROUP)):
+        stop = min(start + GROUP, chunks)
+        for i in range(start, stop):
+            rows = dot(terms[i].reshape(CHUNK, 2 * width), wide, 1, 0)
+            basis[i * CHUNK : (i + 1) * CHUNK, :] = rows[:, :width] + rows[:, width:]
+        rows = pl.ds(start * CHUNK, (stop - start) * CHUNK)
+        copies.append(pltpu.make_async_copy(basis.at[rows], basis_out.at[rows], basis_sem.at[k]))
+        copies[-1].start()
     for p in range(members):
         for q in range(parts):
             start = 2 * part_rows * (p * parts + q)
@@ -157,15 +165,7 @@
                 loads = two_term_loads(sums[q, p], units[q, p], wide) * gene_scale
                 loadings[start:stop, :] = loads[: stop - start]
     copies.append(pltpu.make_async_copy(loadings, load_out, load_sem))
-    copies[0].start()
-    for k, start in enumerate(range(0, chunks, GROUP)):
-        stop = min(start + GROUP, chunks)
-        for i in range(start, stop):
-            rows = dot(terms[i].reshape(CHUNK, 2 * width), wide, 1, 0)
-            basis[i * CHUNK : (i + 1) * CHUNK, :] = rows[:, :width] + rows[:, width:]
-        rows = pl.ds(start * CHUNK, (stop - start) * CHUNK)
-        copies.append(pltpu.make_async_copy(basis.at[rows], basis_out.at[rows], basis_sem.at[k]))
-        copies[-1].start()
+    copies[-1].start()
     for copy in copies:
         copy.wait()
 

time: 89.2 us -> 89 us (level)
  no operation moved by 1% of the time
where the time goes in v5:
time: 89 us; the launch traced here: 88.9 us
  Pallas kernels  87.1 us (98%)
  local copies, waits for them, and re-layouts  0.94 us (1%)
    pallas_call x1, Pallas kernels, shards(): pl.pallas_call(functools.partial(body, n, m, gene_dev, math.sqrt(cell_cou...  85.2 us
    pallas_call x1, Pallas kernels, shards(): pl.pallas_call(functools.partial(write_body, gene_dev, gene_scale), out_s...  1.96 us

profile of v5, /device:TPU:0, one launch (start us, length us, event | category | flops | bytes accessed | tf_op | source)
XLA Modules:
  0.0 88.9 jit_solution(14964014535727948093)
XLA Ops:
  0.6 0.0 copy-start
  0.6 0.9 %copy-done = bf16[1000,128]{1,0:T(8,128)(2,1)S(1)} copy-done((bf16[1000,128]{1,0:T(8,128)(2,1)S(1)}, bf16[1000,128]{1,0:T(8,128)(2,1)}, u32[]{:S(2)}) %copy-start) | copy-done | bytes 256024
  1.6 85.2 %shard_map.41 = (bf16[19,2,128,256]{3,2,1,0:T(8,128)(2,1)S(1)}, bf16[256,256]{1,0:T(8,128)(2,1)S(1)}, s32[2,4,64,128]{3,2,1,0:T(8,128)S(1)}, f32[2,4,1,128]{3,2,1,0:T(1,128)S(1)}) custom-call(s32[1000,4864]{1,0:T(8,128)} %bitcast.1, bf16[1000,128]{1,0:T(8,128)(2,1)S(1)} %copy-done), custom_call_target="tpu_custom_call" | custom-call | tf_op jit(solution)/shard_map/pallas_call | solution.py:647
  86.7 2.0 %shard_map.42 = (f32[4864,128]{1,0:T(8,128)}, f32[1000,128]{1,0:T(8,128)}) custom-call(bf16[19,2,128,256]{3,2,1,0:T(8,128)(2,1)S(1)} %get-tuple-element.6.terms, bf16[256,256]{1,0:T(8,128)(2,1)S(1)} %get-tuple-element.7.wide_ref, s32[2,4,64,128]{3,2,1,0:T(8,128)S(1)} %get-tuple-element.8.sums, f32[2,4,1,128]{3,2,1,0:T(1,128)S(1)} %get-tuple-element.9.units), custom_call_target="tpu_custom_call" | custom-call | tf_op jit(solution)/shard_map/pallas_call | solution.py:657
Async XLA Ops:
  0.6 0.9 %copy-start = (bf16[1000,128]{1,0:T(8,128)(2,1)S(1)}, bf16[1000,128]{1,0:T(8,128)(2,1)}, u32[]{:S(2)}) copy-start(bf16[1000,128]{1,0:T(8,128)(2,1)} %sketch_ref.1) | copy-start | bytes 768004
